TPU v7x, 256 devices: a whole 4x4x8 slice. The times are simulated.
256 devices in a mesh: gx: 2 (over y_lo), gy: 32 (over y_hi, z, core), gz: 4 (over x).
Axes of the slice: x: 4, y: 4 (y_hi: 2, y_lo: 2; y = y_hi * 2 + y_lo), z: 8, core: 2. Of those that a mesh axis runs over, the one named last changes fastest.
Arguments:
- velocity: float32 [3, 256, 256, 512], P(None, 'gy', 'gx', 'gz'), may hold values from -6 to 6
- stress: float32 [6, 256, 256, 512], P(None, 'gy', 'gx', 'gz'), may hold values from -6 to 6
- buoyancy: float32 [256, 256, 512], P('gy', 'gx', 'gz'), may hold values from 0.5 to 2
- stiff_xx: float32 [256, 256, 512], P('gy', 'gx', 'gz'), may hold values from 2 to 4
- stiff_xz: float32 [256, 256, 512], P('gy', 'gx', 'gz'), may hold values from 0.5 to 1
- stiff_zz: float32 [256, 256, 512], P('gy', 'gx', 'gz'), may hold values from 1.5 to 3
- shear_vert: float32 [256, 256, 512], P('gy', 'gx', 'gz'), may hold values from 0.5 to 1
- shear_horiz: float32 [256, 256, 512], P('gy', 'gx', 'gz'), may hold values from 0.6 to 1.2
- prestress: float32 [2, 256, 512], P(None, 'gy', 'gz'), may hold values from -24 to 24
- fault_mask: int32 [256, 512], P('gy', 'gz'), may hold values 0 or 1
- region_ids: int32 [256, 512], P('gy', 'gz'), may hold values from 0 to 7
- inverse_rate: float32 [256, 512], P('gy', 'gz'), may hold values from 100 to 10000
- slip_prev: float32 [256, 512], P('gy', 'gz'), may hold values from 0.01 to 2
- region_a: float32 [8], replicated, may hold values from 0.01 to 0.04
- region_normal: float32 [8], replicated, may hold values from 20 to 60
Outputs:
- new_velocity: float32 [3, 256, 256, 512], P(None, 'gy', 'gx', 'gz')
- new_stress: float32 [6, 256, 256, 512], P(None, 'gy', 'gx', 'gz')
- slip_rate: float32 [256, 512], P('gy', 'gz')
All inputs are finite; a program needn't handle non-finite values. No bound on the sum of `fault_mask` on one device may be relied on, other than what follows from the above.
Results may differ from a plain program's by a relative error of at most 0.0003.
Values sent between devices are 32-bit elements; how exact they have to be, the bound alone decides.
A program may use at most 128 MiB of HBM per device.

v0:
```python
import jax
import jax.numpy as jnp
from jax import lax
from jax.sharding import PartitionSpec as P

STEPS = 3
NEWTON = 3


step_dt = 0.2


def from_behind(shard, axis, by):
    devices = lax.axis_size(axis)
    pairs = [(i, i + by) for i in range(devices) if 0 <= i + by < devices]
    return lax.ppermute(shard, axis, pairs)


def swapped(shard, axis, apart):
    return lax.ppermute(shard, axis, [(i, i ^ 1 << apart) for i in range(lax.axis_size(axis))])


def inverse_sinh(values):
    size_abs = jnp.abs(values)
    return jnp.sign(values) * jnp.log(size_abs + jnp.sqrt(size_abs * size_abs + 1.0))


def local_lower(values):
    beneath = jnp.concatenate([jnp.zeros_like(values[:, :1]), values[:, :-1]], axis=1)
    return values - beneath


def local_upper(values):
    overhead = jnp.concatenate([values[:, 1:], jnp.zeros_like(values[:, :1])], axis=1)
    return overhead - values


def lower_strike(values, beneath):
    return values - jnp.concatenate([beneath, values[:-1]], axis=0)


def upper_strike(values, overhead):
    return jnp.concatenate([values[1:], overhead], axis=0) - values


def lower_dip(values, beneath):
    return values - jnp.concatenate([beneath, values[:, :, :-1]], axis=2)


def upper_dip(values, overhead):
    return jnp.concatenate([values[:, :, 1:], overhead], axis=2) - values


def friction(
    minus_side,
    plus_side,
    minus_buoy,
    plus_buoy,
    prestress,
    fault_mask,
    region_ids,
    inverse_rate,
    slip_prev,
    region_a,
    region_normal,
):
    impedance = 1.0 / (step_dt * (minus_buoy + plus_buoy))
    jump_vec = plus_side - minus_side
    normal_part = impedance * jump_vec[0]
    locked_y = prestress[0] + impedance * jump_vec[1]
    locked_z = prestress[1] + impedance * jump_vec[2]
    magnitude = jnp.sqrt(locked_y * locked_y + locked_z * locked_z + 1.0)
    labels = jnp.arange(region_a.shape[0], dtype=jnp.int32)
    picked = (region_ids[None] == labels[:, None, None]).astype(jnp.float32)
    strength = jnp.sum(picked * region_a[:, None, None], axis=0) * jnp.sum(
        picked * region_normal[:, None, None], axis=0
    )
    velocity_slip = slip_prev
    for turn in range(NEWTON):
        scaled = inverse_rate * velocity_slip
        residual = magnitude - impedance * velocity_slip - strength * inverse_sinh(scaled)
        tangent = -impedance - strength * inverse_rate / jnp.sqrt(1.0 + scaled * scaled)
        velocity_slip = velocity_slip - residual / tangent
    velocity_slip = velocity_slip * fault_mask.astype(jnp.float32)
    retained = 1.0 - impedance * velocity_slip / magnitude
    traction = jnp.stack(
        [normal_part, retained * locked_y - prestress[0], retained * locked_z - prestress[1]]
    )
    return (traction, velocity_slip)


def solve_pair(
    is_minus,
    own_plane,
    other_plane,
    own_buoy,
    other_buoy,
    prestress,
    fault_mask,
    region_ids,
    inverse_rate,
    slip_prev,
    region_a,
    region_normal,
):
    minus_side = jnp.where(is_minus, own_plane, other_plane)
    plus_side = jnp.where(is_minus, other_plane, own_plane)
    minus_buoy = jnp.where(is_minus, own_buoy, other_buoy)
    plus_buoy = jnp.where(is_minus, other_buoy, own_buoy)
    return friction(
        minus_side,
        plus_side,
        minus_buoy,
        plus_buoy,
        prestress,
        fault_mask,
        region_ids,
        inverse_rate,
        slip_prev,
        region_a,
        region_normal,
    )


def one_step(
    velocity,
    stress,
    buoyancy,
    stiff_xx,
    stiff_xz,
    stiff_zz,
    shear_vert,
    shear_horiz,
    prestress,
    fault_mask,
    region_ids,
    inverse_rate,
    slip_prev,
    region_a,
    region_normal,
):
    depth = velocity.shape[2]
    side = lax.axis_index("gx")
    is_minus = side == 0
    stress_xx, stress_yy, stress_zz, stress_yz, stress_xz, stress_xy = stress
    strike_rims = from_behind(jnp.stack([stress_xy[-1:], stress_yy[-1:], stress_yz[-1:]]), "gy", 1)
    dip_rims = from_behind(
        jnp.stack([stress_xz[:, :, -1:], stress_yz[:, :, -1:], stress_zz[:, :, -1:]]), "gz", 1
    )
    trial_x = velocity[0] + step_dt * buoyancy * (
        local_lower(stress_xx)
        + lower_strike(stress_xy, strike_rims[0])
        + lower_dip(stress_xz, dip_rims[0])
    )
    trial_y = velocity[1] + step_dt * buoyancy * (
        local_lower(stress_xy)
        + lower_strike(stress_yy, strike_rims[1])
        + lower_dip(stress_yz, dip_rims[1])
    )
    trial_z = velocity[2] + step_dt * buoyancy * (
        local_lower(stress_xz)
        + lower_strike(stress_yz, strike_rims[2])
        + lower_dip(stress_zz, dip_rims[2])
    )
    trial = jnp.stack([trial_x, trial_y, trial_z])
    own_plane = jnp.where(is_minus, trial[:, :, depth - 1, :], trial[:, :, 0, :])
    own_buoy = jnp.where(is_minus, buoyancy[:, depth - 1, :], buoyancy[:, 0, :])
    marker = (jnp.arange(depth, dtype=jnp.int32) == jnp.where(is_minus, depth - 1, 0)).astype(
        jnp.float32
    )
    other_plane, other_buoy = swapped((own_plane, own_buoy), "gx", 0)
    traction, slip_rate = solve_pair(
        is_minus,
        own_plane,
        other_plane,
        own_buoy,
        other_buoy,
        prestress,
        fault_mask,
        region_ids,
        inverse_rate,
        slip_prev,
        region_a,
        region_normal,
    )
    sign = jnp.where(is_minus, 1.0, -1.0)
    correction = sign * (step_dt * own_buoy * traction)
    spread = marker[None, None, :, None]
    moved = trial + spread * correction[:, :, None, :]
    strike_next = from_behind(moved[:, 0:1], "gy", -1)
    dip_next = from_behind(moved[:, :, :, 0:1], "gz", -1)
    moved_x, moved_y, moved_z = moved
    strain_xx = local_upper(moved_x)
    strain_yy = upper_strike(moved_y, strike_next[1])
    strain_zz = upper_dip(moved_z, dip_next[2])
    lame = stiff_xx - 2.0 * shear_horiz
    new_xx = stress_xx + step_dt * (stiff_xx * strain_xx + lame * strain_yy + stiff_xz * strain_zz)
    new_yy = stress_yy + step_dt * (lame * strain_xx + stiff_xx * strain_yy + stiff_xz * strain_zz)
    new_zz = stress_zz + step_dt * (stiff_xz * (strain_xx + strain_yy) + stiff_zz * strain_zz)
    new_yz = stress_yz + step_dt * shear_vert * (
        upper_dip(moved_y, dip_next[1]) + upper_strike(moved_z, strike_next[2])
    )
    new_xz = stress_xz + step_dt * shear_vert * (
        upper_dip(moved_x, dip_next[0]) + local_upper(moved_z)
    )
    new_xy = stress_xy + step_dt * shear_horiz * (
        upper_strike(moved_x, strike_next[0]) + local_upper(moved_y)
    )
    return (moved, jnp.stack([new_xx, new_yy, new_zz, new_yz, new_xz, new_xy]), slip_rate)


def local(
    velocity,
    stress,
    buoyancy,
    stiff_xx,
    stiff_xz,
    stiff_zz,
    shear_vert,
    shear_horiz,
    prestress,
    fault_mask,
    region_ids,
    inverse_rate,
    slip_prev,
    region_a,
    region_normal,
):
    slip_rate = slip_prev
    for count in range(STEPS):
        velocity, stress, slip_rate = one_step(
            velocity,
            stress,
            buoyancy,
            stiff_xx,
            stiff_xz,
            stiff_zz,
            shear_vert,
            shear_horiz,
            prestress,
            fault_mask,
            region_ids,
            inverse_rate,
            slip_rate,
            region_a,
            region_normal,
        )
    return (velocity, stress, slip_rate)


def solution(mesh):
    in_specs = (
        P(None, "gy", "gx", "gz"),
        P(None, "gy", "gx", "gz"),
        P("gy", "gx", "gz"),
        P("gy", "gx", "gz"),
        P("gy", "gx", "gz"),
        P("gy", "gx", "gz"),
        P("gy", "gx", "gz"),
        P("gy", "gx", "gz"),
        P(None, "gy", "gz"),
        P("gy", "gz"),
        P("gy", "gz"),
        P("gy", "gz"),
        P("gy", "gz"),
        P(),
        P(),
    )
    out_specs = (P(None, "gy", "gx", "gz"), P(None, "gy", "gx", "gz"), P("gy", "gz"))
    return jax.shard_map(local, mesh=mesh, in_specs=in_specs, out_specs=out_specs, check_vma=False)
```

profile of v0, /device:TPU:229, one launch (start us, length us, event | category | flops | bytes accessed | tf_op | source)
XLA Modules:
  0.0 173.6 jit_solution(1095776244455093055)
XLA Ops:
  0.6 3.4 %fusion.128 = (f32[1,8,128,128]{3,2,1,0:T(8,128)}, f32[8,128,128]{2,1,0:T(8,128)}, f32[1,8,128,128]{3,2,1,0:T(8,128)}, f32[1,8,128,128]{3,2,1,0:T(8,128)S(1)}, f...) fusion(f32[6,8,128,128]{3,2,1,0:T(8,128)} %param.16), kind=kLoop, calls=%fused_computation.290 | loop fusion | bytes 6815744 | tf_op jit(solution)/shard_map/unstack | solution.py:145
  4.7 2.8 %collective-permute-start.1 = (f32[3,8,128,1]{2,1,3,0:T(8,128)S(1)}, f32[3,8,128,1]{2,1,3,0:T(8,128)S(1)}, u32[]{:S(2)}, u32[]{:S(2)}) collective-permute-start(f32[3,8,128,1]{2,1,3,0:T(8,128)S(1)} %pad_maximum_fusion.7), channel_id=1, source_target_pairs={{0,1},{1,2},{2,3},{4,5},{5,6},{6,7},{8,9},{9,10},{10,11},{12,13},{... | collective-permute-start | bytes 36872 | tf_op jit(solution)/shard_map/ppermute | solution.py:16
  8.5 2.5 %collective-permute-start = (f32[3,1,128,128]{3,2,1,0:T(8,128)S(1)}, f32[3,1,128,128]{3,2,1,0:T(8,128)}, u32[]{:S(2)}, u32[]{:S(2)}) collective-permute-start(f32[3,1,128,128]{3,2,1,0:T(8,128)S(1)} %pad_maximum_fusion.4), channel_id=1, source_target_pairs={{0,4},{4,8},{8,12},{12,16},{16,20},{20,24},{24,28},{28,32},{32,36}... | collective-permute-start | bytes 589832 | tf_op jit(solution)/shard_map/ppermute | solution.py:16
  12.6 2.5 %fusion.129 = (f32[1,7,128,128]{3,2,1,0:T(8,128)}, f32[1,7,128,128]{3,2,1,0:T(8,128)}, f32[1,7,128,128]{3,2,1,0:T(8,128)}) fusion(f32[6,8,128,128]{3,2,1,0:T(8,128)} %param.16), kind=kLoop, calls=%fused_computation.291 | loop fusion | bytes 2752512 | tf_op jit(solution)/shard_map/slice | solution.py:39
  15.1 2.7 %fusion.133 = (f32[1,8,128,128]{3,2,1,0:T(8,128)}, f32[1,8,128,128]{3,2,1,0:T(8,128)}, f32[1,8,128,128]{3,2,1,0:T(8,128)}) fusion(f32[3,8,128,128]{3,2,1,0:T(8,128)} %param.15), kind=kLoop, calls=%fused_computation.295 | loop fusion | bytes 3145728 | tf_op jit(solution)/shard_map/slice | solution.py:150
  18.3 1.5 copy.781
  22.9 1.4 copy.847
  24.3 2.2 %copy.848 = f32[1,8,128,128]{2,3,1,0:T(8,128)} copy(f32[1,8,128,128]{3,2,1,0:T(8,128)} %get-tuple-element.58) | data formatting | bytes 1048576
  26.5 2.0 %copy.854 = f32[1,8,128,128]{2,3,1,0:T(8,128)} copy(f32[1,8,128,128]{3,2,1,0:T(8,128)} %get-tuple-element.54) | data formatting | bytes 1048576
  28.6 2.0 %copy.846 = f32[1,8,128,128]{2,3,1,0:T(8,128)} copy(f32[1,8,128,128]{3,2,1,0:T(8,128)} %get-tuple-element.91) | data formatting | bytes 1048576
  30.6 2.1 %copy.853 = f32[1,8,128,128]{2,3,1,0:T(8,128)} copy(f32[1,8,128,128]{3,2,1,0:T(8,128)} %get-tuple-element.92) | data formatting | bytes 1048576
  32.7 2.0 %copy.855 = f32[1,7,128,128]{2,3,1,0:T(8,128)} copy(f32[1,7,128,128]{3,2,1,0:T(8,128)} %get-tuple-element.61) | data formatting | bytes 917504
  34.7 2.0 %copy.849 = f32[1,7,128,128]{2,3,1,0:T(8,128)} copy(f32[1,7,128,128]{3,2,1,0:T(8,128)} %get-tuple-element.59) | data formatting | bytes 917504
  36.7 2.0 %copy.764 = f32[8,128,128]{1,2,0:T(8,128)} copy(f32[8,128,128]{2,1,0:T(8,128)} %get-tuple-element.53) | data formatting | bytes 1048576 | tf_op jit(solution)/shard_map/unstack | solution.py:145
  38.7 2.0 %copy.856 = f32[1,8,128,128]{2,3,1,0:T(8,128)} copy(f32[1,8,128,128]{3,2,1,0:T(8,128)} %get-tuple-element.93) | data formatting | bytes 1048576
  40.8 2.0 %copy.857 = f32[1,7,128,128]{2,3,1,0:T(8,128)} copy(f32[1,7,128,128]{3,2,1,0:T(8,128)} %get-tuple-element.60) | data formatting | bytes 917504
  44.1 2.0 %fusion.17 = f32[1,8,128,128]{2,3,1,0:T(8,128)S(1)} fusion(f32[7,128,128]{1,2,0:T(8,128)} %bitcast.508, f32[1,128,128]{1,2,0:T(8,128)S(1)} %copy.761, f32[8,128,128]{1,2,0:T(8,128)} %copy.764, f32[8,128,127]{1,2,0:T(8,128)} %bitcast.498, f32[8,128,1]{1,2,0:T(1,128)S(1)} %bitcast.533, f32[1,8,128,128]{2,3,1,0:T(8,128)} %copy.856, ...), kind=kLoop, calls=%fused_computation.41 | loop fusion | flops 1310720 | bytes 4714496 | tf_op jit(solution)/shard_map/stack | solution.py:165
  46.4 1.6 fusion.7
  51.9 2.1 %copy.776 = f32[8,128,128]{1,2,0:T(8,128)} copy(f32[8,128,128]{2,1,0:T(8,128)} %param.22) | data formatting | bytes 1048576 | tf_op args[7]
  54.0 2.1 %copy.774 = f32[8,128,128]{1,2,0:T(8,128)} copy(f32[8,128,128]{2,1,0:T(8,128)} %param.19) | data formatting | bytes 1048576 | tf_op args[4]
  56.1 2.0 %copy.792 = f32[8,128,128]{1,2,0:T(8,128)} copy(f32[8,128,128]{2,1,0:T(8,128)} %param.20) | data formatting | bytes 1048576 | tf_op args[5]
  58.3 1.5 multiply_add_fusion.1
  60.0 2.5 %collective-permute-start.5 = (f32[3,8,128,1]{2,3,1,0:T(1,128)S(1)}, f32[3,8,128,1]{2,3,1,0:T(1,128)S(1)}, u32[]{:S(2)}, u32[]{:S(2)}) collective-permute-start(f32[3,8,128,1]{2,3,1,0:T(1,128)S(1)} %slice.662), channel_id=1, source_target_pairs={{1,0},{2,1},{3,2},{5,4},{6,5},{7,6},{9,8},{10,9},{11,10},{13,12},{... | collective-permute-start | bytes 36872 | tf_op jit(solution)/shard_map/ppermute | solution.py:16
  63.3 3.3 %collective-permute-start.4 = (f32[3,1,128,128]{2,3,1,0:T(8,128)S(1)}, f32[3,1,128,128]{2,3,1,0:T(8,128)S(1)}, u32[]{:S(2)}, u32[]{:S(2)}) collective-permute-start(f32[3,1,128,128]{2,3,1,0:T(8,128)S(1)} %slice.659), channel_id=1, source_target_pairs={{4,0},{8,4},{12,8},{16,12},{20,16},{24,20},{28,24},{32,28},{36,32}... | collective-permute-start | bytes 589832 | tf_op jit(solution)/shard_map/ppermute | solution.py:16
  66.7 7.2 %collective-permute-done.4 = f32[3,1,128,128]{2,3,1,0:T(8,128)S(1)} collective-permute-done((f32[3,1,128,128]{2,3,1,0:T(8,128)S(1)}, f32[3,1,128,128]{2,3,1,0:T(8,128)S(1)}, u32[]{:S(2)}, u32[]{:S(2)}) %collective-permute-start.4) | collective-permute-done | bytes 196640 | tf_op jit(solution)/shard_map/ppermute | solution.py:16
  76.0 1.7 multiply_add_fusion.3
  79.5 2.8 %collective-permute-start.7 = (f32[3,8,128,1]{2,1,3,0:T(8,128)S(1)}, f32[3,8,128,1]{2,1,3,0:T(8,128)S(1)}, u32[]{:S(2)}, u32[]{:S(2)}) collective-permute-start(f32[3,8,128,1]{2,1,3,0:T(8,128)S(1)} %pad_maximum_fusion.8), channel_id=1, source_target_pairs={{0,1},{1,2},{2,3},{4,5},{5,6},{6,7},{8,9},{9,10},{10,11},{12,13},{... | collective-permute-start | bytes 36872 | tf_op jit(solution)/shard_map/ppermute | solution.py:16
  82.5 2.2 %collective-permute-start.6 = (f32[3,1,128,128]{2,3,1,0:T(8,128)S(1)}, f32[3,1,128,128]{2,3,1,0:T(8,128)S(1)}, u32[]{:S(2)}, u32[]{:S(2)}) collective-permute-start(f32[3,1,128,128]{2,3,1,0:T(8,128)S(1)} %pad_maximum_fusion.5), channel_id=1, source_target_pairs={{0,4},{4,8},{8,12},{12,16},{16,20},{20,24},{24,28},{28,32},{32,36}... | collective-permute-start | bytes 589832 | tf_op jit(solution)/shard_map/ppermute | solution.py:16
  84.8 2.5 %collective-permute-done.6 = f32[3,1,128,128]{2,3,1,0:T(8,128)S(1)} collective-permute-done((f32[3,1,128,128]{2,3,1,0:T(8,128)S(1)}, f32[3,1,128,128]{2,3,1,0:T(8,128)S(1)}, u32[]{:S(2)}, u32[]{:S(2)}) %collective-permute-start.6) | collective-permute-done | bytes 196640 | tf_op jit(solution)/shard_map/ppermute | solution.py:16
  92.7 2.2 %copy.821 = f32[8,128,128]{1,0,2:T(8,128)} copy(f32[8,128,128]{2,1,0:T(8,128)} %param.20) | data formatting | bytes 1048576 | tf_op args[5]
  95.1 1.5 multiply_add_fusion
  96.8 2.5 %collective-permute-start.10 = (f32[3,8,128,1]{2,3,1,0:T(1,128)S(1)}, f32[3,8,128,1]{2,3,1,0:T(1,128)S(1)}, u32[]{:S(2)}, u32[]{:S(2)}) collective-permute-start(f32[3,8,128,1]{2,3,1,0:T(1,128)S(1)} %slice.706), channel_id=1, source_target_pairs={{1,0},{2,1},{3,2},{5,4},{6,5},{7,6},{9,8},{10,9},{11,10},{13,12},{... | collective-permute-start | bytes 36872 | tf_op jit(solution)/shard_map/ppermute | solution.py:16
  101.4 2.6 %collective-permute-start.9 = (f32[3,1,128,128]{2,3,1,0:T(8,128)S(1)}, f32[3,1,128,128]{2,3,1,0:T(8,128)S(1)}, u32[]{:S(2)}, u32[]{:S(2)}) collective-permute-start(f32[3,1,128,128]{2,3,1,0:T(8,128)S(1)} %slice.703), channel_id=1, source_target_pairs={{4,0},{8,4},{12,8},{16,12},{20,16},{24,20},{28,24},{32,28},{36,32}... | collective-permute-start | bytes 589832 | tf_op jit(solution)/shard_map/ppermute | solution.py:16
  104.1 10.0 %collective-permute-done.9 = f32[3,1,128,128]{2,3,1,0:T(8,128)S(1)} collective-permute-done((f32[3,1,128,128]{2,3,1,0:T(8,128)S(1)}, f32[3,1,128,128]{2,3,1,0:T(8,128)S(1)}, u32[]{:S(2)}, u32[]{:S(2)}) %collective-permute-start.9) | collective-permute-done | bytes 196640 | tf_op jit(solution)/shard_map/ppermute | solution.py:16
  114.2 3.4 %fusion.52 = (f32[8,128,128]{1,0,2:T(8,128)S(1)}, f32[8,128,128]{1,0,2:T(8,128)S(1)}, f32[8,128,128]{1,0,2:T(8,128)S(1)}) fusion(f32[8,128,1]{1,0,2:T(8,128)S(1)} %bitcast.526, f32[8,128,127]{1,0,2:T(8,128)S(1)} %slice.721, f32[8,128,128]{1,2,0:T(8,128)S(1)} %copy-done.7, f32[8,127,128]{1,0,2:T(8,128)S(1)} %slice.723, ...), kind=kLoop, calls=%fused_computation.96 | loop fusion | flops 2228224 | bytes 8904704 | tf_op jit(solution)/shard_map/add | solution.py:203
  117.8 1.4 copy_add_fusion.4
  120.5 2.8 %collective-permute-start.12 = (f32[3,8,128,1]{2,1,3,0:T(8,128)S(1)}, f32[3,8,128,1]{2,1,3,0:T(8,128)S(1)}, u32[]{:S(2)}, u32[]{:S(2)}) collective-permute-start(f32[3,8,128,1]{2,1,3,0:T(8,128)S(1)} %pad_maximum_fusion.9), channel_id=1, source_target_pairs={{0,1},{1,2},{2,3},{4,5},{5,6},{6,7},{8,9},{9,10},{10,11},{12,13},{... | collective-permute-start | bytes 36872 | tf_op jit(solution)/shard_map/ppermute | solution.py:16
  123.6 2.2 %collective-permute-start.11 = (f32[3,1,128,128]{2,3,1,0:T(8,128)S(1)}, f32[3,1,128,128]{2,3,1,0:T(8,128)S(1)}, u32[]{:S(2)}, u32[]{:S(2)}) collective-permute-start(f32[3,1,128,128]{2,3,1,0:T(8,128)S(1)} %pad_maximum_fusion.6), channel_id=1, source_target_pairs={{0,4},{4,8},{8,12},{12,16},{16,20},{20,24},{24,28},{28,32},{32,36}... | collective-permute-start | bytes 589832 | tf_op jit(solution)/shard_map/ppermute | solution.py:16
  125.8 2.6 %collective-permute-done.11 = f32[3,1,128,128]{2,3,1,0:T(8,128)S(1)} collective-permute-done((f32[3,1,128,128]{2,3,1,0:T(8,128)S(1)}, f32[3,1,128,128]{2,3,1,0:T(8,128)S(1)}, u32[]{:S(2)}, u32[]{:S(2)}) %collective-permute-start.11) | collective-permute-done | bytes 196640 | tf_op jit(solution)/shard_map/ppermute | solution.py:16
  129.3 1.4 fusion.49
  132.3 2.5 %collective-permute-done.13 = f32[3,8,128]{2,1,0:T(8,128)S(1)} collective-permute-done((f32[3,8,128]{2,1,0:T(8,128)S(1)}, f32[3,8,128]{2,1,0:T(8,128)S(1)}, u32[]{:S(2)}, u32[]{:S(2)}) %collective-permute-start.13) | collective-permute-done | bytes 12320 | tf_op jit(solution)/shard_map/ppermute | solution.py:20
  138.2 2.5 %collective-permute-start.15 = (f32[3,8,128,1]{2,1,3,0:T(8,128)S(1)}, f32[3,8,128,1]{2,1,3,0:T(8,128)S(1)}, u32[]{:S(2)}, u32[]{:S(2)}) collective-permute-start(f32[3,8,128,1]{2,1,3,0:T(8,128)S(1)} %slice.749), channel_id=1, source_target_pairs={{1,0},{2,1},{3,2},{5,4},{6,5},{7,6},{9,8},{10,9},{11,10},{13,12},{... | collective-permute-start | bytes 36872 | tf_op jit(solution)/shard_map/ppermute | solution.py:16
  144.6 1.6 copy.839
  146.2 2.2 %collective-permute-start.14 = (f32[3,1,128,128]{2,3,1,0:T(8,128)S(1)}, f32[3,1,128,128]{2,3,1,0:T(8,128)S(1)}, u32[]{:S(2)}, u32[]{:S(2)}) collective-permute-start(f32[3,1,128,128]{2,3,1,0:T(8,128)S(1)} %bitcast.519), channel_id=1, source_target_pairs={{4,0},{8,4},{12,8},{16,12},{20,16},{24,20},{28,24},{32,28},{36,32}... | collective-permute-start | bytes 589832 | tf_op jit(solution)/shard_map/ppermute | solution.py:16
  148.4 10.6 %collective-permute-done.14 = f32[3,1,128,128]{2,3,1,0:T(8,128)S(1)} collective-permute-done((f32[3,1,128,128]{2,3,1,0:T(8,128)S(1)}, f32[3,1,128,128]{2,3,1,0:T(8,128)S(1)}, u32[]{:S(2)}, u32[]{:S(2)}) %collective-permute-start.14) | collective-permute-done | bytes 196640 | tf_op jit(solution)/shard_map/ppermute | solution.py:16
  159.1 3.1 %bitcast_dynamic-update-slice_fusion.2 = (f32[6,8,128,128]{2,1,3,0:T(8,128)}, f32[8,128,128]{1,0,2:T(8,128)S(1)}) fusion(f32[8,128,128]{1,0,2:T(8,128)} %copy-done.23, f32[8,128,128]{1,0,2:T(8,128)} %copy-done, f32[8,128,128]{1,0,2:T(8,128)} %copy-done.2, f32[3,8,128,128]{2,1,3,0:T(8,128)S(1)} %copy_add_fusion, f32[8,127,128]{1,0,2:T(8,128)} %slice.744, ...), kind=kLoop, calls=%fused_computation.135 | loop fusion | flops 1835007 | bytes 6287360
  168.7 1.4 fusion.77
  170.1 3.5 %copy.840 = f32[6,8,128,128]{3,2,1,0:T(8,128)} copy(f32[6,8,128,128]{2,1,3,0:T(8,128)} %fusion.77) | data formatting | bytes 6291456
  (293 shorter events, 42.5 us)
Async XLA Ops:
  4.7 10.4 %copy-start.52 = (f32[1,8,128,128]{2,1,3,0:T(8,128)}, f32[1,8,128,128]{2,1,3,0:T(8,128)S(1)}, u32[]{:S(2)}) copy-start(f32[1,8,128,128]{2,1,3,0:T(8,128)S(1)} %copy.852) | copy-start | bytes 1572868
  4.7 38.0 %collective-permute-start.1 = (f32[3,8,128,1]{2,1,3,0:T(8,128)S(1)}, f32[3,8,128,1]{2,1,3,0:T(8,128)S(1)}, u32[]{:S(2)}, u32[]{:S(2)}) collective-permute-start(f32[3,8,128,1]{2,1,3,0:T(8,128)S(1)} %pad_maximum_fusion.7), channel_id=1, source_target_pairs={{0,1},{1,2},{2,3},{4,5},{5,6},{6,7},{8,9},{9,10},{10,11},{12,13},{... | collective-permute-start | bytes 36872 | tf_op jit(solution)/shard_map/ppermute | solution.py:16
  8.5 34.3 %collective-permute-start = (f32[3,1,128,128]{3,2,1,0:T(8,128)S(1)}, f32[3,1,128,128]{3,2,1,0:T(8,128)}, u32[]{:S(2)}, u32[]{:S(2)}) collective-permute-start(f32[3,1,128,128]{3,2,1,0:T(8,128)S(1)} %pad_maximum_fusion.4), channel_id=1, source_target_pairs={{0,4},{4,8},{8,12},{12,16},{16,20},{20,24},{24,28},{28,32},{32,36}... | collective-permute-start | bytes 589832 | tf_op jit(solution)/shard_map/ppermute | solution.py:16
  11.8 46.3 %collective-permute-start.2 = (f32[8,128]{1,0:T(8,128)S(1)}, f32[8,128]{1,0:T(8,128)S(1)}, u32[]{:S(2)}, u32[]{:S(2)}) collective-permute-start(f32[8,128]{1,0:T(8,128)S(1)} %get-tuple-element.38), channel_id=1, source_target_pairs={{0,128},{128,0},{1,129},{129,1},{2,130},{130,2},{3,131},{131,3},{4... | collective-permute-start | bytes 12296 | tf_op jit(solution)/shard_map/ppermute | solution.py:20
  18.3 101.0 %copy-start = (f32[8,128,128]{1,0,2:T(8,128)}, f32[8,128,128]{1,0,2:T(8,128)S(1)}, u32[]{:S(2)}) copy-start(f32[8,128,128]{1,0,2:T(8,128)S(1)} %copy.769) | copy-start | bytes 1572868
  22.8 23.3 %copy-start.13 = (f32[8,128,128]{1,2,0:T(8,128)}, f32[8,128,128]{1,2,0:T(8,128)S(1)}, u32[]{:S(2)}) copy-start(f32[8,128,128]{1,2,0:T(8,128)S(1)} %copy.744) | copy-start | bytes 1572868
  24.3 21.8 %copy-start.19 = (f32[1,8,128,128]{2,3,1,0:T(8,128)}, f32[1,8,128,128]{2,3,1,0:T(8,128)S(1)}, u32[]{:S(2)}) copy-start(f32[1,8,128,128]{2,3,1,0:T(8,128)S(1)} %copy.847) | copy-start | bytes 1572868
  50.0 8.1 %collective-permute-start.3 = (f32[3,8,128]{2,1,0:T(8,128)S(1)}, f32[3,8,128]{2,1,0:T(8,128)S(1)}, u32[]{:S(2)}, u32[]{:S(2)}) collective-permute-start(f32[3,8,128]{2,1,0:T(8,128)S(1)} %fusion.1), channel_id=1, source_target_pairs={{0,128},{128,0},{1,129},{129,1},{2,130},{130,2},{3,131},{131,3},{4... | collective-permute-start | bytes 36872 | tf_op jit(solution)/shard_map/ppermute | solution.py:20
  51.8 6.3 %copy-start.68 = (f32[2,8,128]{2,1,0:T(8,128)S(1)}, f32[2,8,128]{2,1,0:T(8,128)}, u32[]{:S(2)}) copy-start(f32[2,8,128]{2,1,0:T(8,128)} %param.23) | copy-start | bytes 24580
  51.8 6.3 %copy-start.69 = (s32[8,128]{1,0:T(8,128)S(1)}, s32[8,128]{1,0:T(8,128)}, u32[]{:S(2)}) copy-start(s32[8,128]{1,0:T(8,128)} %param.24) | copy-start | bytes 12292
  51.8 6.3 %copy-start.70 = (f32[8,128]{1,0:T(8,128)S(1)}, f32[8,128]{1,0:T(8,128)}, u32[]{:S(2)}) copy-start(f32[8,128]{1,0:T(8,128)} %param.26) | copy-start | bytes 12292
  51.8 6.3 %copy-start.71 = (f32[8,128]{1,0:T(8,128)S(1)}, f32[8,128]{1,0:T(8,128)}, u32[]{:S(2)}) copy-start(f32[8,128]{1,0:T(8,128)} %param.27) | copy-start | bytes 12292
  51.8 6.5 %copy-start.41 = (f32[1,8,128,128]{2,3,1,0:T(8,128)S(1)}, f32[1,8,128,128]{2,3,1,0:T(8,128)}, u32[]{:S(2)}) copy-start(f32[1,8,128,128]{2,3,1,0:T(8,128)} %copy-done.40) | copy-start | bytes 1572868
  51.9 6.5 %copy-start.43 = (f32[1,8,128,128]{2,3,1,0:T(8,128)S(1)}, f32[1,8,128,128]{2,3,1,0:T(8,128)}, u32[]{:S(2)}) copy-start(f32[1,8,128,128]{2,3,1,0:T(8,128)} %copy-done.42) | copy-start | bytes 1572868
  60.0 6.7 %collective-permute-start.5 = (f32[3,8,128,1]{2,3,1,0:T(1,128)S(1)}, f32[3,8,128,1]{2,3,1,0:T(1,128)S(1)}, u32[]{:S(2)}, u32[]{:S(2)}) collective-permute-start(f32[3,8,128,1]{2,3,1,0:T(1,128)S(1)} %slice.662), channel_id=1, source_target_pairs={{1,0},{2,1},{3,2},{5,4},{6,5},{7,6},{9,8},{10,9},{11,10},{13,12},{... | collective-permute-start | bytes 36872 | tf_op jit(solution)/shard_map/ppermute | solution.py:16
  63.0 10.9 %copy-start.54 = (f32[8,128,128]{1,0,2:T(8,128)S(1)}, f32[8,128,128]{1,0,2:T(8,128)}, u32[]{:S(2)}) copy-start(f32[8,128,128]{1,0,2:T(8,128)} %broadcast_multiply_fusion.3) | copy-start | bytes 1572868
  63.3 10.6 %collective-permute-start.4 = (f32[3,1,128,128]{2,3,1,0:T(8,128)S(1)}, f32[3,1,128,128]{2,3,1,0:T(8,128)S(1)}, u32[]{:S(2)}, u32[]{:S(2)}) collective-permute-start(f32[3,1,128,128]{2,3,1,0:T(8,128)S(1)} %slice.659), channel_id=1, source_target_pairs={{4,0},{8,4},{12,8},{16,12},{20,16},{24,20},{28,24},{32,28},{36,32}... | collective-permute-start | bytes 589832 | tf_op jit(solution)/shard_map/ppermute | solution.py:16
  74.6 13.2 %copy-start.6 = (f32[8,128,128]{1,2,0:T(8,128)}, f32[8,128,128]{1,2,0:T(8,128)S(1)}, u32[]{:S(2)}) copy-start(f32[8,128,128]{1,2,0:T(8,128)S(1)} %get-tuple-element.67) | copy-start | bytes 1572868
  77.7 10.1 %copy-start.4 = (f32[8,128,128]{1,2,0:T(8,128)}, f32[8,128,128]{1,2,0:T(8,128)S(1)}, u32[]{:S(2)}) copy-start(f32[8,128,128]{1,2,0:T(8,128)S(1)} %get-tuple-element.84) | copy-start | bytes 1572868
  77.7 10.1 %copy-start.17 = (f32[8,128,128]{1,2,0:T(8,128)}, f32[8,128,128]{1,2,0:T(8,128)S(1)}, u32[]{:S(2)}) copy-start(f32[8,128,128]{1,2,0:T(8,128)S(1)} %get-tuple-element.35) | copy-start | bytes 1572868
  78.2 9.1 %copy-start.29 = (f32[8,128,128]{1,2,0:T(8,128)}, f32[8,128,128]{1,2,0:T(8,128)S(1)}, u32[]{:S(2)}) copy-start(f32[8,128,128]{1,2,0:T(8,128)S(1)} %get-tuple-element.49) | copy-start | bytes 1572868
  79.4 8.3 %copy-start.25 = (f32[8,128,128]{1,0,2:T(8,128)}, f32[8,128,128]{1,0,2:T(8,128)S(1)}, u32[]{:S(2)}) copy-start(f32[8,128,128]{1,0,2:T(8,128)S(1)} %copy_add_fusion.5) | copy-start | bytes 1572868
  79.5 5.3 %collective-permute-start.7 = (f32[3,8,128,1]{2,1,3,0:T(8,128)S(1)}, f32[3,8,128,1]{2,1,3,0:T(8,128)S(1)}, u32[]{:S(2)}, u32[]{:S(2)}) collective-permute-start(f32[3,8,128,1]{2,1,3,0:T(8,128)S(1)} %pad_maximum_fusion.8), channel_id=1, source_target_pairs={{0,1},{1,2},{2,3},{4,5},{5,6},{6,7},{8,9},{9,10},{10,11},{12,13},{... | collective-permute-start | bytes 36872 | tf_op jit(solution)/shard_map/ppermute | solution.py:16
  82.4 4.9 %copy-start.14 = (f32[8,128,128]{1,2,0:T(8,128)S(1)}, f32[8,128,128]{1,2,0:T(8,128)}, u32[]{:S(2)}) copy-start(f32[8,128,128]{1,2,0:T(8,128)} %copy-done.13) | copy-start | bytes 1572868
  82.5 4.8 %collective-permute-start.6 = (f32[3,1,128,128]{2,3,1,0:T(8,128)S(1)}, f32[3,1,128,128]{2,3,1,0:T(8,128)S(1)}, u32[]{:S(2)}, u32[]{:S(2)}) collective-permute-start(f32[3,1,128,128]{2,3,1,0:T(8,128)S(1)} %pad_maximum_fusion.5), channel_id=1, source_target_pairs={{0,4},{4,8},{8,12},{12,16},{16,20},{20,24},{24,28},{28,32},{32,36}... | collective-permute-start | bytes 589832 | tf_op jit(solution)/shard_map/ppermute | solution.py:16
  90.6 4.5 %copy-start.45 = (f32[1,8,128,128]{2,3,1,0:T(8,128)S(1)}, f32[1,8,128,128]{2,3,1,0:T(8,128)}, u32[]{:S(2)}) copy-start(f32[1,8,128,128]{2,3,1,0:T(8,128)} %copy-done.44) | copy-start | bytes 1572868
  90.6 4.5 %copy-start.47 = (f32[1,8,128,128]{2,3,1,0:T(8,128)S(1)}, f32[1,8,128,128]{2,3,1,0:T(8,128)}, u32[]{:S(2)}) copy-start(f32[1,8,128,128]{2,3,1,0:T(8,128)} %copy-done.46) | copy-start | bytes 1572868
  90.6 4.3 %collective-permute-start.8 = (f32[3,8,128]{2,1,0:T(8,128)S(1)}, f32[3,8,128]{2,1,0:T(8,128)S(1)}, u32[]{:S(2)}, u32[]{:S(2)}) collective-permute-start(f32[3,8,128]{2,1,0:T(8,128)S(1)} %fusion), channel_id=1, source_target_pairs={{0,128},{128,0},{1,129},{129,1},{2,130},{130,2},{3,131},{131,3},{4... | collective-permute-start | bytes 36872 | tf_op jit(solution)/shard_map/ppermute | solution.py:20
  92.7 26.5 %copy-start.2 = (f32[8,128,128]{1,0,2:T(8,128)}, f32[8,128,128]{1,0,2:T(8,128)S(1)}, u32[]{:S(2)}) copy-start(f32[8,128,128]{1,0,2:T(8,128)S(1)} %copy.806) | copy-start | bytes 1572868
  96.8 7.3 %collective-permute-start.10 = (f32[3,8,128,1]{2,3,1,0:T(1,128)S(1)}, f32[3,8,128,1]{2,3,1,0:T(1,128)S(1)}, u32[]{:S(2)}, u32[]{:S(2)}) collective-permute-start(f32[3,8,128,1]{2,3,1,0:T(1,128)S(1)} %slice.706), channel_id=1, source_target_pairs={{1,0},{2,1},{3,2},{5,4},{6,5},{7,6},{9,8},{10,9},{11,10},{13,12},{... | collective-permute-start | bytes 36872 | tf_op jit(solution)/shard_map/ppermute | solution.py:16
  101.4 12.8 %copy-start.5 = (f32[8,128,128]{1,2,0:T(8,128)S(1)}, f32[8,128,128]{1,2,0:T(8,128)}, u32[]{:S(2)}) copy-start(f32[8,128,128]{1,2,0:T(8,128)} %copy-done.4) | copy-start | bytes 1572868
  101.4 12.8 %copy-start.7 = (f32[8,128,128]{1,2,0:T(8,128)S(1)}, f32[8,128,128]{1,2,0:T(8,128)}, u32[]{:S(2)}) copy-start(f32[8,128,128]{1,2,0:T(8,128)} %copy-done.6) | copy-start | bytes 1572868
  101.4 12.8 %copy-start.11 = (f32[8,128,128]{1,0,2:T(8,128)S(1)}, f32[8,128,128]{1,0,2:T(8,128)}, u32[]{:S(2)}) copy-start(f32[8,128,128]{1,0,2:T(8,128)} %copy-done.10) | copy-start | bytes 1572868
  101.4 12.8 %copy-start.32 = (f32[8,128,128]{1,2,0:T(8,128)S(1)}, f32[8,128,128]{1,2,0:T(8,128)}, u32[]{:S(2)}) copy-start(f32[8,128,128]{1,2,0:T(8,128)} %get-tuple-element.143) | copy-start | bytes 1572868
  101.4 12.6 %collective-permute-start.9 = (f32[3,1,128,128]{2,3,1,0:T(8,128)S(1)}, f32[3,1,128,128]{2,3,1,0:T(8,128)S(1)}, u32[]{:S(2)}, u32[]{:S(2)}) collective-permute-start(f32[3,1,128,128]{2,3,1,0:T(8,128)S(1)} %slice.703), channel_id=1, source_target_pairs={{4,0},{8,4},{12,8},{16,12},{20,16},{24,20},{28,24},{32,28},{36,32}... | collective-permute-start | bytes 589832 | tf_op jit(solution)/shard_map/ppermute | solution.py:16
  114.2 3.5 %copy-start.18 = (f32[8,128,128]{1,2,0:T(8,128)S(1)}, f32[8,128,128]{1,2,0:T(8,128)}, u32[]{:S(2)}) copy-start(f32[8,128,128]{1,2,0:T(8,128)} %copy-done.17) | copy-start | bytes 1572868
  117.7 11.6 %copy-start.8 = (f32[8,128,128]{1,0,2:T(8,128)}, f32[8,128,128]{1,0,2:T(8,128)S(1)}, u32[]{:S(2)}) copy-start(f32[8,128,128]{1,0,2:T(8,128)S(1)} %get-tuple-element.96) | copy-start | bytes 1572868
  119.2 10.0 %copy-start.23 = (f32[8,128,128]{1,0,2:T(8,128)}, f32[8,128,128]{1,0,2:T(8,128)S(1)}, u32[]{:S(2)}) copy-start(f32[8,128,128]{1,0,2:T(8,128)S(1)} %get-tuple-element.28) | copy-start | bytes 1572868
  120.5 8.0 %copy-start.15 = (f32[8,128,128]{1,0,2:T(8,128)}, f32[8,128,128]{1,0,2:T(8,128)S(1)}, u32[]{:S(2)}) copy-start(f32[8,128,128]{1,0,2:T(8,128)S(1)} %get-tuple-element.51) | copy-start | bytes 1572868
  120.5 8.8 %copy-start.27 = (f32[8,128,128]{1,0,2:T(8,128)}, f32[8,128,128]{1,0,2:T(8,128)S(1)}, u32[]{:S(2)}) copy-start(f32[8,128,128]{1,0,2:T(8,128)S(1)} %get-tuple-element.50) | copy-start | bytes 1572868
  120.5 5.3 %collective-permute-start.12 = (f32[3,8,128,1]{2,1,3,0:T(8,128)S(1)}, f32[3,8,128,1]{2,1,3,0:T(8,128)S(1)}, u32[]{:S(2)}, u32[]{:S(2)}) collective-permute-start(f32[3,8,128,1]{2,1,3,0:T(8,128)S(1)} %pad_maximum_fusion.9), channel_id=1, source_target_pairs={{0,1},{1,2},{2,3},{4,5},{5,6},{6,7},{8,9},{9,10},{10,11},{12,13},{... | collective-permute-start | bytes 36872 | tf_op jit(solution)/shard_map/ppermute | solution.py:16
  123.5 4.9 %copy-start.34 = (f32[8,128,128]{1,2,0:T(8,128)S(1)}, f32[8,128,128]{1,2,0:T(8,128)}, u32[]{:S(2)}) copy-start(f32[8,128,128]{1,2,0:T(8,128)} %get-tuple-element.101) | copy-start | bytes 1572868
  123.6 4.8 %collective-permute-start.11 = (f32[3,1,128,128]{2,3,1,0:T(8,128)S(1)}, f32[3,1,128,128]{2,3,1,0:T(8,128)S(1)}, u32[]{:S(2)}, u32[]{:S(2)}) collective-permute-start(f32[3,1,128,128]{2,3,1,0:T(8,128)S(1)} %pad_maximum_fusion.6), channel_id=1, source_target_pairs={{0,4},{4,8},{8,12},{12,16},{16,20},{20,24},{24,28},{28,32},{32,36}... | collective-permute-start | bytes 589832 | tf_op jit(solution)/shard_map/ppermute | solution.py:16
  131.9 2.9 %collective-permute-start.13 = (f32[3,8,128]{2,1,0:T(8,128)S(1)}, f32[3,8,128]{2,1,0:T(8,128)S(1)}, u32[]{:S(2)}, u32[]{:S(2)}) collective-permute-start(f32[3,8,128]{2,1,0:T(8,128)S(1)} %fusion.2), channel_id=1, source_target_pairs={{0,128},{128,0},{1,129},{129,1},{2,130},{130,2},{3,131},{131,3},{4... | collective-permute-start | bytes 36872 | tf_op jit(solution)/shard_map/ppermute | solution.py:20
  138.2 10.2 %collective-permute-start.15 = (f32[3,8,128,1]{2,1,3,0:T(8,128)S(1)}, f32[3,8,128,1]{2,1,3,0:T(8,128)S(1)}, u32[]{:S(2)}, u32[]{:S(2)}) collective-permute-start(f32[3,8,128,1]{2,1,3,0:T(8,128)S(1)} %slice.749), channel_id=1, source_target_pairs={{1,0},{2,1},{3,2},{5,4},{6,5},{7,6},{9,8},{10,9},{11,10},{13,12},{... | collective-permute-start | bytes 36872 | tf_op jit(solution)/shard_map/ppermute | solution.py:16
  146.2 12.8 %collective-permute-start.14 = (f32[3,1,128,128]{2,3,1,0:T(8,128)S(1)}, f32[3,1,128,128]{2,3,1,0:T(8,128)S(1)}, u32[]{:S(2)}, u32[]{:S(2)}) collective-permute-start(f32[3,1,128,128]{2,3,1,0:T(8,128)S(1)} %bitcast.519), channel_id=1, source_target_pairs={{4,0},{8,4},{12,8},{16,12},{20,16},{24,20},{28,24},{32,28},{36,32}... | collective-permute-start | bytes 589832 | tf_op jit(solution)/shard_map/ppermute | solution.py:16
  159.0 3.2 %copy-start.1 = (f32[8,128,128]{1,0,2:T(8,128)S(1)}, f32[8,128,128]{1,0,2:T(8,128)}, u32[]{:S(2)}) copy-start(f32[8,128,128]{1,0,2:T(8,128)} %copy-done) | copy-start | bytes 1572868
  159.0 3.2 %copy-start.3 = (f32[8,128,128]{1,0,2:T(8,128)S(1)}, f32[8,128,128]{1,0,2:T(8,128)}, u32[]{:S(2)}) copy-start(f32[8,128,128]{1,0,2:T(8,128)} %copy-done.2) | copy-start | bytes 1572868
  (43 other events, 73.6 us)
where the time goes:
time: 175 us; the launch traced here: 174 us
  local copies, waits for them, and re-layouts  67.2 us (38%)
  waiting for transfers between devices  35.4 us (20%)
  other arithmetic  35.1 us (20%)
  starting transfers between devices  33.6 us (19%)
  between operations  2.32 us (1%)
    unnamed x175, local copies, waits for them, and re-layouts  43.8 us
    ppermute x12, waiting for transfers between devices, from_behind(): return lax.ppermute(shard, axis, pairs)  32.8 us
    ppermute x12, starting transfers between devices, from_behind(): return lax.ppermute(shard, axis, pairs)  30.8 us
    another operation x9, other arithmetic, one_step(): trial = jnp.stack([trial_x, trial_y, trial_z])  7.42 us
    unnamed x4, other arithmetic  6.28 us
    another operation x2, local copies, waits for them, and re-layouts, one_step(): stress_xx, stress_yy, stress_zz, stress_yz, stress_xz, stress_xy = stress  5.44 us
    add x3, other arithmetic, one_step(): moved = trial + spread * correction[:, :, None, :]  4.05 us
    add x2, other arithmetic, one_step(): stress_xz + step_dt * shear_vert * (upper_dip(moved_x, dip_next[0]) + loc...  3.96 us
  transfers between devices with their start and end apart: 16, of which 6 were waited for; matrix products, arithmetic and copies ran while one was open for 33% of the time, Pallas kernels for 0%

commit v1 on v0

v1 whole, which is shorter than its diff:
```python
import functools

import jax
import jax.numpy as jnp
from jax import lax
from jax.experimental import pallas as pl
from jax.experimental.pallas import tpu as pltpu
from jax.sharding import PartitionSpec as P

STEPS = 3
NEWTON = 3
DT = 0.2
MESH = pl.DeviceIdType.MESH

S_ORDER = (0, 2, 4, 3, 1, 5)
XX, ZZ, XZ, YZ, YY, XY = range(6)
BUO, C11, C66, C13, C44, C33 = range(6)

PLANES = 8
ROWS = 128
TILES = 17
EXT = 8 * TILES
GHOST = slice(ROWS, EXT)


def kernel(
    vel_hbm, str_hbm, buo_hbm, c11_hbm, c13_hbm, c33_hbm, c44_hbm, c66_hbm,
    pre_hbm, mask_hbm, ids_hbm, inv_hbm, slip_hbm, reg_a_hbm, reg_n_hbm,
    vel_out, str_out, slip_out,
    S, V, C, VN, VP, PK, ZN, ZM, ZD1, ZD2, PI, ZI, UN, UM, UO, UD1, UD2, SG, CG,
    FB, SE, VE, CE, pre, mask, ids, inv, slip, strength, reg_a, reg_n,
    lsem, ssem, rsem,
):
    f32 = jnp.float32
    ngy, ngz = lax.axis_size("gy"), lax.axis_size("gz")
    gx, gy, gz = lax.axis_index("gx"), lax.axis_index("gy"), lax.axis_index("gz")
    is_minus = gx == 0
    lane = lax.broadcasted_iota(jnp.int32, (8, 128), 1)
    sub = lax.broadcasted_iota(jnp.int32, (8, 128), 0)
    edge = (1 - gx) * (ROWS - 8)
    own_f = (1 - gx) * (ROWS - 1)
    other_f = ROWS + gx * 7

    up_y, dn_y, up_z, dn_z = gy < ngy - 1, gy > 0, gz < ngz - 1, gz > 0

    def at(dx, dy, dz):
        return (
            gx if dx == 0 else 1 - gx,
            jnp.clip(gy + dy, 0, ngy - 1),
            jnp.clip(gz + dz, 0, ngz - 1),
        )

    def exists(dy, dz):
        ok = gy >= 0
        if dy:
            ok = jnp.logical_and(ok, up_y if dy > 0 else dn_y)
        if dz:
            ok = jnp.logical_and(ok, up_z if dz > 0 else dn_z)
        return ok

    barrier = pltpu.get_barrier_semaphore()
    around = [
        (0, 1, 0), (0, -1, 0), (0, 0, 1), (0, 0, -1), (0, -1, 1), (0, 1, -1),
        (1, 0, 0), (1, 1, 0), (1, -1, 0), (1, 0, 1), (1, 0, -1),
    ]
    count = jnp.int32(0)
    for dx, dy, dz in around:
        ok = exists(dy, dz)
        count = count + ok.astype(jnp.int32)

        @pl.when(ok)
        def _():
            pl.semaphore_signal(barrier, inc=1, device_id=at(dx, dy, dz), device_id_type=MESH)

    loads = {}

    def load(name, src, dst):
        copy = pltpu.make_async_copy(src, dst, lsem.at[len(loads)])
        copy.start()
        loads[name] = copy

    own = pl.ds(0, ROWS)
    edge_rows = pl.ds(pl.multiple_of(edge, 8), 8)
    for i in range(6):
        load(("se", i), str_hbm.at[S_ORDER[i], :, edge_rows], SE.at[i])
    load("ve", vel_hbm.at[:, :, edge_rows], VE)
    coefficients = ((BUO, buo_hbm), (C11, c11_hbm), (C66, c66_hbm), (C13, c13_hbm), (C44, c44_hbm), (C33, c33_hbm))
    for i, ref in coefficients:
        load(("ce", i), ref.at[:, edge_rows], CE.at[i])
    for i in (YZ, YY, XY):
        load(("s7", i), str_hbm.at[S_ORDER[i], PLANES - 1], S.at[i, PLANES, own])
    for i in (ZZ, XZ):
        load(("s", i), str_hbm.at[S_ORDER[i]], S.at[i, pl.ds(1, PLANES), own])
    for i in (YZ, YY, XY):
        load(("s", i), str_hbm.at[S_ORDER[i], pl.ds(0, PLANES - 1)], S.at[i, pl.ds(1, PLANES - 1), own])
    load(("s", XX), str_hbm.at[S_ORDER[XX]], S.at[XX, pl.ds(1, PLANES), own])
    load("v", vel_hbm, V.at[:, :, own])
    for i, ref in coefficients:
        load(i, ref, C.at[i, pl.ds(1, PLANES), own])
    load("pre", pre_hbm, pre)
    load("mask", mask_hbm, mask)
    load("ids", ids_hbm, ids)
    load("inv", inv_hbm, inv)
    load("slip", slip_hbm, slip)
    load("reg_a", reg_a_hbm, reg_a)
    load("reg_n", reg_n_hbm, reg_n)

    sent = {}

    def message(name, src, dst, dx, dy, dz):
        i = len(sent)
        copy = pltpu.make_async_remote_copy(
            src_ref=src, dst_ref=dst, send_sem=ssem.at[i], recv_sem=rsem.at[i],
            device_id=at(dx, dy, dz), device_id_type=MESH,
        )
        sent[name] = [copy, exists(dy, dz), exists(-dy, -dz), True]

        @pl.when(exists(dy, dz))
        def _():
            copy.start()

    def arrived(name):
        copy, _, source, _ = sent[name]

        @pl.when(source)
        def _():
            copy.wait_recv()

    def gone(name):
        copy, target, _, pending = sent[name]
        if pending:
            sent[name][3] = False

            @pl.when(target)
            def _():
                copy.wait_send()

    def rows(t):
        return pl.ds(8 * t, 8)

    def below(ref, lead, t):
        if t in (0, TILES - 1):
            return jnp.where(sub == 0, 0.0, pltpu.roll(ref[lead + (rows(t),)], 1, 0))
        return ref[lead + (pl.ds(8 * t - 1, 8),)]

    def above(ref, lead, t):
        if t in (TILES - 2, TILES - 1):
            return jnp.where(sub == 7, 0.0, pltpu.roll(ref[lead + (rows(t),)], 7, 0))
        return ref[lead + (pl.ds(8 * t + 1, 8),)]

    def pack(ref, lead, plane0, out, tiles):
        groups = (tiles + 1) // 2

        def body(c, accs):
            accs = list(accs)
            for y in range(PLANES):
                for t in range(tiles):
                    base = 64 * (t % 2) + 16 * c + 2 * y
                    moved = pltpu.roll(ref[lead + c, plane0 + y, rows(t)], base + 1, 1)
                    hit = jnp.logical_or(lane == base, lane == base + 1)
                    accs[t // 2] = jnp.where(hit, moved, accs[t // 2])
            return tuple(accs)

        accs = lax.fori_loop(0, 3, body, tuple(jnp.zeros((8, 128), f32) for _ in range(groups)))
        for g in range(groups):
            out[pl.ds(8 * g, 8)] = accs[g]
        return accs

    def unpack(src, dst):
        for t in range(TILES):
            tile = src[pl.ds(8 * (t // 2), 8)]
            dst[rows(t)] = tile if t % 2 == 0 else pltpu.roll(tile, 64, 1)

    def trial(y, tiles):
        back = lax.rem(128 - 2 * y, 128)

        def lower_dip(value, i, t):
            halo = pltpu.roll(SG[i, rows(t)], back, 1)
            return value - jnp.where(lane == 0, halo, pltpu.roll(value, 1, 1))

        for t in tiles:
            r = rows(t)
            sxx, szz, sxz, syz, syy, sxy = (S[i, y + 1, r] for i in range(6))
            scale = DT * C[BUO, y + 1, r]
            vx = V[0, y, r] + scale * (
                (sxx - below(S, (XX, y + 1), t)) + (sxy - S[XY, y, r]) + lower_dip(sxz, 1, t)
            )
            vy = V[1, y, r] + scale * (
                (sxy - below(S, (XY, y + 1), t)) + (syy - S[YY, y, r]) + lower_dip(syz, 2, t)
            )
            vz = V[2, y, r] + scale * (
                (sxz - below(S, (XZ, y + 1), t)) + (syz - S[YZ, y, r]) + lower_dip(szz, 0, t)
            )
            V[0, y, r] = vx
            V[1, y, r] = vy
            V[2, y, r] = vz

    def stress(p, here, here_lead, over, over_lead, halo, halo_y, ghost=False, last=False):
        def put(i, value):
            if last:
                str_out[S_ORDER[i], p - 1, r] = value
            else:
                S[i, p, r] = value

        for t in range(TILES - 1 if last else TILES):
            r = rows(t)

            def upper_dip(value, c):
                edge_column = pltpu.roll(halo[r], 126 - 16 * c - 2 * halo_y, 1)
                return jnp.where(lane == 127, edge_column, pltpu.roll(value, 127, 1)) - value

            vx, vy, vz = (here[here_lead(c) + (r,)] for c in range(3))
            ox, oy, oz = (over[over_lead(c) + (r,)] for c in range(3))
            exx = above(here, here_lead(0), t) - vx
            eyy = oy - vy
            ezz = upper_dip(vz, 2)
            c11, c66, c13, c44 = (C[i, p, r] for i in (C11, C66, C13, C44))
            lame = c11 - 2.0 * c66
            put(YY, S[YY, p, r] + DT * (lame * exx + c11 * eyy + c13 * ezz))
            put(YZ, S[YZ, p, r] + DT * c44 * (upper_dip(vy, 1) + (oz - vz)))
            put(XY, S[XY, p, r] + DT * c66 * ((ox - vx) + (above(here, here_lead(1), t) - vy)))
            if not ghost:
                put(XX, S[XX, p, r] + DT * (c11 * exx + lame * eyy + c13 * ezz))
                put(ZZ, S[ZZ, p, r] + DT * (c13 * (exx + eyy) + C[C33, p, r] * ezz))
                put(XZ, S[XZ, p, r] + DT * c44 * (
                    upper_dip(vx, 0) + (above(here, here_lead(2), t) - vz)
                ))

    def stress_own(k, y):
        stress(y + 1, V, lambda c: (c, y), V, lambda c: (c, y + 1), UN, y, last=k == STEPS - 1)

    def stress_last(k):
        stress(PLANES, V, lambda c: (c, PLANES - 1), VN, lambda c: (k, c), UN, PLANES - 1, last=k == STEPS - 1)

    def stress_ghost(k):
        stress(0, VP, lambda c: (k, c), V, lambda c: (c, 0), UD2, PLANES - 1, ghost=True)

    def column_ghost():
        for t in range(TILES):
            r = rows(t)

            def shifted(ref, by):
                return pltpu.roll(ref[r], by % 128, 1)

            def upper_rows(c):
                if t in (TILES - 2, TILES - 1):
                    return pltpu.roll(
                        jnp.where(sub == 7, 0.0, pltpu.roll(UM[r], 7, 0)), (-16 * c) % 128, 1
                    )
                return pltpu.roll(UM[pl.ds(8 * t + 1, 8)], (-16 * c) % 128, 1)

            def next_strike(value, c):
                corner = shifted(UD1, 14 - 16 * c)
                return jnp.where(lane == 14, corner, pltpu.roll(value, 126, 1))

            vx, vy, vz = UM[r], shifted(UM, -16), shifted(UM, -32)
            ox, oy, oz = shifted(UO, -1), shifted(UO, -17), shifted(UO, -33)
            exx = upper_rows(0) - vx
            eyy = next_strike(vy, 1) - vy
            ezz = oz - vz
            c13, c44, c33 = CG[0, r], CG[1, r], CG[2, r]
            SG[0, r] = SG[0, r] + DT * (c13 * (exx + eyy) + c33 * ezz)
            SG[1, r] = SG[1, r] + DT * c44 * ((ox - vx) + (upper_rows(2) - vz))
            SG[2, r] = SG[2, r] + DT * c44 * ((oy - vy) + (next_strike(vz, 2) - vz))

    def fault():
        for c in range(3):
            for y in range(PLANES):
                FB[c, pl.ds(y, 1)] = V[c, y, pl.ds(own_f, 1)]
                FB[3 + c, pl.ds(y, 1)] = V[c, y, pl.ds(other_f, 1)]
        own_v, other_v = [FB[c] for c in range(3)], [FB[3 + c] for c in range(3)]
        own_b, other_b = FB[6], FB[7]
        minus_b = jnp.where(is_minus, own_b, other_b)
        plus_b = jnp.where(is_minus, other_b, own_b)
        minus_v = [jnp.where(is_minus, a, b) for a, b in zip(own_v, other_v)]
        plus_v = [jnp.where(is_minus, b, a) for a, b in zip(own_v, other_v)]
        impedance = 1.0 / (DT * (minus_b + plus_b))
        jump = [b - a for a, b in zip(minus_v, plus_v)]
        locked_y = pre[0] + impedance * jump[1]
        locked_z = pre[1] + impedance * jump[2]
        magnitude = jnp.sqrt(locked_y * locked_y + locked_z * locked_z + 1.0)
        hold = strength[...]
        rate = inv[...]
        value = slip[...]
        for _ in range(NEWTON):
            scaled = rate * value
            size = jnp.abs(scaled)
            root = jnp.sqrt(size * size + 1.0)
            log = jnp.log(size + root)
            residual = magnitude - impedance * value - hold * jnp.where(scaled < 0.0, -log, log)
            tangent = -impedance - hold * rate / root
            value = value - residual / tangent
        value = value * mask[...].astype(f32)
        slip[...] = value
        retained = 1.0 - impedance * value / magnitude
        traction = [impedance * jump[0], retained * locked_y - pre[0], retained * locked_z - pre[1]]
        for c in range(3):
            minus_new = minus_v[c] + DT * minus_b * traction[c]
            plus_new = plus_v[c] - DT * plus_b * traction[c]
            FB[c] = jnp.where(is_minus, minus_new, plus_new)
            FB[3 + c] = jnp.where(is_minus, plus_new, minus_new)
        for c in range(3):
            for y in range(PLANES):
                V[c, y, pl.ds(own_f, 1)] = FB[c, pl.ds(y, 1)]
                V[c, y, pl.ds(other_f, 1)] = FB[3 + c, pl.ds(y, 1)]

    @pl.when(jnp.logical_not(up_y))
    def _():
        VN[...] = jnp.zeros(VN.shape, f32)
        ZD1[...] = jnp.zeros(ZD1.shape, f32)

    @pl.when(jnp.logical_not(dn_y))
    def _():
        S[pl.ds(YZ, 3), 0] = jnp.zeros((3, EXT, 128), f32)

    @pl.when(jnp.logical_not(up_z))
    def _():
        ZN[...] = jnp.zeros(ZN.shape, f32)
        ZD2[...] = jnp.zeros(ZD2.shape, f32)

    @pl.when(jnp.logical_not(dn_z))
    def _():
        SG[...] = jnp.zeros(SG.shape, f32)

    ghost_rows = pl.ds(ROWS, 8)
    every = pl.ds(1, PLANES)
    strike = pl.ds(YZ, 3)
    strike_c = pl.ds(C11, 4)
    rest = pl.ds(C11, 5)
    for i in (YZ, YY, XY):
        loads["s7", i].wait()
    for i in range(6):
        loads["se", i].wait()
    loads["ve"].wait()
    for i in range(6):
        loads["ce", i].wait()
    pl.semaphore_wait(barrier, count)
    message("y0", S.at[strike, PLANES, own], S.at[strike, 0, own], 0, 1, 0)
    message("xy0", SE.at[strike, PLANES - 1], S.at[strike, 0, ghost_rows], 1, 1, 0)
    message("x0", SE, S.at[:, every, ghost_rows], 1, 0, 0)
    message("xv", VE, V.at[:, :, ghost_rows], 1, 0, 0)
    message("xb", CE.at[BUO], C.at[BUO, every, ghost_rows], 1, 0, 0)
    for i in (ZZ, XZ, YZ, YY, XY, XX):
        loads["s", i].wait()
    accs = pack(S, ZZ, 1, PI.at[0], 16)
    message("z0", PI.at[0, pl.ds(0, 64)], ZI.at[0, pl.ds(0, 64)], 0, 0, 1)
    PI[0, pl.ds(64, 8)] = jnp.where(is_minus, pltpu.roll(accs[7], 64, 1), accs[0])
    message("xz0", PI.at[0, pl.ds(64, 8)], ZI.at[0, pl.ds(64, 8)], 1, 0, 1)
    loads["v"].wait()
    for i in range(6):
        loads[i].wait()
    message("xc", CE.at[rest], C.at[rest, every, ghost_rows], 1, 0, 0)
    message("yc", C.at[strike_c, PLANES, own], C.at[strike_c, 0, own], 0, 1, 0)
    message("xyc", CE.at[strike_c, PLANES - 1], C.at[strike_c, 0, ghost_rows], 1, 1, 0)
    accs = pack(C, C13, 1, PI.at[1], 16)
    message("zc", PI.at[1, pl.ds(0, 64)], ZI.at[1, pl.ds(0, 64)], 0, 0, 1)
    PI[1, pl.ds(64, 8)] = jnp.where(is_minus, pltpu.roll(accs[7], 64, 1), accs[0])
    message("xzc", PI.at[1, pl.ds(64, 8)], ZI.at[1, pl.ds(64, 8)], 1, 0, 1)

    for name in ("pre", "mask", "ids", "inv", "slip", "reg_a", "reg_n"):
        loads[name].wait()
    number = ids[...]
    picked_a = jnp.zeros((8, 128), f32)
    picked_n = jnp.zeros((8, 128), f32)
    for i in range(8):
        picked_a = jnp.where(number == i, reg_a[i], picked_a)
        picked_n = jnp.where(number == i, reg_n[i], picked_n)
    strength[...] = picked_a * picked_n

    def columns(src, dst):
        for t in range(TILES):
            tile = src[pl.ds(8 * (t // 2), 8)]
            for c in range(3):
                shift = (-16 * c - 64 * (t % 2)) % 128
                dst[c, rows(t)] = pltpu.roll(tile, shift, 1) if shift else tile

    arrived("z0")
    arrived("xz0")

    @pl.when(dn_z)
    def _():
        columns(ZI.at[0], SG)

    own_tiles = range(TILES - 1)
    all_tiles = range(TILES)

    def planes(first, last, body):
        def step(y, carry):
            body(y)
            return carry

        lax.fori_loop(first, last, step, 0)

    planes(1, PLANES, lambda y: trial(y, own_tiles))
    arrived("x0")
    arrived("xv")
    arrived("xb")
    arrived("xy0")
    for y in range(PLANES):
        FB[6, pl.ds(y, 1)] = C[BUO, y + 1, pl.ds(own_f, 1)]
        FB[7, pl.ds(y, 1)] = C[BUO, y + 1, pl.ds(other_f, 1)]
    planes(0, PLANES, lambda y: trial(y, [TILES - 1]))
    arrived("y0")
    planes(0, 1, lambda y: trial(y, own_tiles))

    for k in range(STEPS):
        last = k == STEPS - 1
        fault()
        message(("yb", k), V.at[:, 0], VN.at[k], 0, -1, 0)
        if not last:
            message(("yf", k), V.at[:, PLANES - 1], VP.at[k], 0, 1, 0)
        else:
            slip_out[...] = slip[...]

            def copy_plane(y):
                for c in range(3):
                    vel_out[c, y] = V[c, y, own]

            planes(0, PLANES, copy_plane)
        pack(V, 0, 0, PK.at[k], TILES)
        message(("zb", k), PK.at[k], ZN.at[k], 0, 0, -1)
        if not last:
            message(("zf", k), PK.at[k], ZM.at[k], 0, 0, 1)
            message(("d1", k), PK.at[k], ZD1.at[k], 0, -1, 1)
            message(("d2", k), PK.at[k], ZD2.at[k], 0, 1, -1)
        if k == 0:
            arrived("zc")
            arrived("xzc")

            @pl.when(dn_z)
            def _():
                columns(ZI.at[1], CG)

            arrived("xc")
            gone("y0")
        arrived(("zb", k))
        unpack(ZN.at[k], UN)
        planes(0, PLANES - 1, functools.partial(stress_own, k))
        if last:
            arrived(("yb", k))
            planes(0, 1, lambda y: stress_last(k))
            break
        arrived(("zf", k))
        arrived(("d1", k))

        @pl.when(dn_z)
        def _():
            unpack(ZM.at[k], UM)
            unpack(ZD1.at[k], UD1)
            unpack(PK.at[k], UO)
            column_ghost()

        planes(1, PLANES - 1, lambda y: trial(y, all_tiles))
        if k == 0:
            arrived("yc")
            arrived("xyc")
        arrived(("d2", k))
        arrived(("yf", k))

        @pl.when(dn_y)
        def _():
            unpack(ZD2.at[k], UD2)
            stress_ghost(k)

        arrived(("yb", k))
        gone(("yb", k))
        gone(("yf", k))
        planes(0, 1, lambda y: stress_last(k))
        planes(0, 2, lambda i: trial((PLANES - 1) * i, all_tiles))

    for name in list(sent):
        gone(name)


def local(
    velocity, stress, buoyancy, stiff_xx, stiff_xz, stiff_zz, shear_vert, shear_horiz,
    prestress, fault_mask, region_ids, inverse_rate, slip_prev, region_a, region_normal,
):
    f32 = jnp.float32
    hbm = pl.BlockSpec(memory_space=pltpu.HBM)
    vmem = pl.BlockSpec(memory_space=pltpu.VMEM)
    tile = pltpu.VMEM((8, 128), f32)
    plane = (EXT, 128)
    packed = (72, 128)
    large = [
        pltpu.with_memory_space_constraint(x, pltpu.HBM)
        for x in (
            velocity, stress, buoyancy, stiff_xx, stiff_xz, stiff_zz, shear_vert, shear_horiz,
            prestress, fault_mask, region_ids, inverse_rate, slip_prev, region_a, region_normal,
        )
    ]
    return pl.pallas_call(
        kernel,
        out_shape=(
            jax.ShapeDtypeStruct(velocity.shape, f32),
            jax.ShapeDtypeStruct(stress.shape, f32),
            jax.ShapeDtypeStruct(slip_prev.shape, f32),
        ),
        in_specs=[hbm] * 15,
        out_specs=(vmem, vmem, vmem),
        scratch_shapes=[
            pltpu.VMEM((6, PLANES + 1) + plane, f32),
            pltpu.VMEM((3, PLANES) + plane, f32),
            pltpu.VMEM((6, PLANES + 1) + plane, f32),
            pltpu.VMEM((STEPS, 3) + plane, f32),
            pltpu.VMEM((STEPS - 1, 3) + plane, f32),
            pltpu.VMEM((STEPS,) + packed, f32),
            pltpu.VMEM((STEPS,) + packed, f32),
            pltpu.VMEM((STEPS - 1,) + packed, f32),
            pltpu.VMEM((STEPS - 1,) + packed, f32),
            pltpu.VMEM((STEPS - 1,) + packed, f32),
            pltpu.VMEM((2,) + packed, f32),
            pltpu.VMEM((2,) + packed, f32),
            pltpu.VMEM(plane, f32),
            pltpu.VMEM(plane, f32),
            pltpu.VMEM(plane, f32),
            pltpu.VMEM(plane, f32),
            pltpu.VMEM(plane, f32),
            pltpu.VMEM((3,) + plane, f32),
            pltpu.VMEM((3,) + plane, f32),
            pltpu.VMEM((8, 8, 128), f32),
            pltpu.VMEM((6, PLANES, 8, 128), f32),
            pltpu.VMEM((3, PLANES, 8, 128), f32),
            pltpu.VMEM((6, PLANES, 8, 128), f32),
            pltpu.VMEM((2, 8, 128), f32),
            pltpu.VMEM((8, 128), jnp.int32),
            pltpu.VMEM((8, 128), jnp.int32),
            tile,
            tile,
            tile,
            pltpu.SMEM((8,), f32),
            pltpu.SMEM((8,), f32),
            pltpu.SemaphoreType.DMA((40,)),
            pltpu.SemaphoreType.DMA((32,)),
            pltpu.SemaphoreType.DMA((32,)),
        ],
        compiler_params=pltpu.CompilerParams(
            collective_id=0, has_side_effects=True, vmem_limit_bytes=40 * 1024 * 1024
        ),
        name="rupture",
    )(*large)


def solution(mesh):
    cell, fault_tile = P("gy", "gx", "gz"), P("gy", "gz")
    field = P(None, "gy", "gx", "gz")
    in_specs = (field, field) + (cell,) * 6 + (P(None, "gy", "gz"),) + (fault_tile,) * 4 + (P(), P())
    out_specs = (field, field, fault_tile)
    return jax.shard_map(local, mesh=mesh, in_specs=in_specs, out_specs=out_specs, check_vma=False)
```

time: 175 us -> 45.8 us (0.26)
  the two profiles are of different devices: /device:TPU:229 before, /device:TPU:1 now
where the time goes in v1:
time: 45.8 us; the launch traced here: 45.1 us
  Pallas kernels  41.1 us (90%)
  local copies, waits for them, and re-layouts  3.4 us (7%)
  between operations  0.65 us (1%)
    pallas_call x1, Pallas kernels, local(): pl.pallas_call(kernel, out_shape=(jax.ShapeDtypeStruct(velocity.shape, f3...  41.1 us
    unnamed x3, local copies, waits for them, and re-layouts  3.4 us

profile of v1, /device:TPU:1, one launch (start us, length us, event | category | flops | bytes accessed | tf_op | source)
XLA Modules:
  0.0 45.1 jit_solution(17970415486314164282)
XLA Ops:
  0.6 41.1 %rupture.1 = (f32[3,8,128,128]{3,2,1,0:T(8,128)S(1)}, f32[6,8,128,128]{3,2,1,0:T(8,128)S(1)}, f32[8,128]{1,0:T(8,128)S(1)}) custom-call(f32[3,8,128,128]{3,2,1,0:T(8,128)} %vel_hbm.1, f32[6,8,128,128]{3,2,1,0:T(8,128)} %str_hbm.1, f32[8,128,128]{2,1,0:T(8,128)} %buo_hbm.1, f32[8,128,128]{2,1,0:T(8,128)} %c11_hbm.1, f32[8,128,128]{2,1,0:T(8,128)} %c13_hbm.1, ...), custom_call_target="tpu_custom_call" | custom-call | tf_op jit(solution)/shard_map/rupture/pallas_call | solution.py:492
  41.7 1.1 %copy.21 = f32[3,8,128,128]{3,2,1,0:T(8,128)} copy(f32[3,8,128,128]{3,2,1,0:T(8,128)S(1)} %get-tuple-element.6) | data formatting | bytes 3145728
  42.9 1.7 %copy.22 = f32[6,8,128,128]{3,2,1,0:T(8,128)} copy(f32[6,8,128,128]{3,2,1,0:T(8,128)S(1)} %get-tuple-element.7) | data formatting | bytes 6291456
  44.5 0.6 %copy.23 = f32[8,128]{1,0:T(8,128)} copy(f32[8,128]{1,0:T(8,128)S(1)} %get-tuple-element.8) | data formatting | bytes 8192

commit v2 on v1

--- a/solution.py
+++ b/solution.py
@@ -27,8 +27,8 @@
     vel_hbm, str_hbm, buo_hbm, c11_hbm, c13_hbm, c33_hbm, c44_hbm, c66_hbm,
     pre_hbm, mask_hbm, ids_hbm, inv_hbm, slip_hbm, reg_a_hbm, reg_n_hbm,
     vel_out, str_out, slip_out,
-    S, V, C, VN, VP, PK, ZN, ZM, ZD1, ZD2, PI, ZI, UN, UM, UO, UD1, UD2, SG, CG,
-    FB, SE, VE, CE, pre, mask, ids, inv, slip, strength, reg_a, reg_n,
+    S, V, C, VN, VP, PK, ZN, ZM, GP, CK, ZD1, ZD2, PI, ZI, UN, UM, UO, SG, CG,
+    FB, SE, VE, CE, XS, XR, pre, mask, ids, inv, slip, strength, reg_a, reg_n,
     lsem, ssem, rsem,
 ):
     f32 = jnp.float32
@@ -148,13 +148,15 @@
             return jnp.where(sub == 7, 0.0, pltpu.roll(ref[lead + (rows(t),)], 7, 0))
         return ref[lead + (pl.ds(8 * t + 1, 8),)]
 
-    def pack(ref, lead, plane0, out, tiles):
+    def pack(ref, lead, plane0, out, tiles, pick=lambda y, t: True):
         groups = (tiles + 1) // 2
 
         def body(c, accs):
             accs = list(accs)
             for y in range(PLANES):
                 for t in range(tiles):
+                    if not pick(y, t):
+                        continue
                     base = 64 * (t % 2) + 16 * c + 2 * y
                     moved = pltpu.roll(ref[lead + c, plane0 + y, rows(t)], base + 1, 1)
                     hit = jnp.logical_or(lane == base, lane == base + 1)
@@ -166,16 +168,52 @@
             out[pl.ds(8 * g, 8)] = accs[g]
         return accs
 
+    FAULT = (0, TILES - 2, TILES - 1)
+    INNER = range(1, TILES - 2)
+
+    def early(y, t):
+        return 0 < y < PLANES - 1 and t in INNER
+
+    def merge(src, dst):
+        strike_index = lax.rem(lane, 16) // 2
+        outer = jnp.logical_or(strike_index == 0, strike_index == PLANES - 1)
+        for g in range((TILES + 1) // 2):
+            late = outer
+            if 2 * g in FAULT:
+                late = jnp.logical_or(late, lane < 64)
+            if 2 * g + 1 in FAULT:
+                late = jnp.logical_or(late, lane >= 64)
+            tile = jnp.where(late, src[1, pl.ds(8 * g, 8)], src[0, pl.ds(8 * g, 8)])
+            dst[rows(2 * g)] = tile
+            if 2 * g + 1 < TILES:
+                dst[rows(2 * g + 1)] = pltpu.roll(tile, 64, 1)
+
     def unpack(src, dst):
         for t in range(TILES):
             tile = src[pl.ds(8 * (t // 2), 8)]
             dst[rows(t)] = tile if t % 2 == 0 else pltpu.roll(tile, 64, 1)
 
+    def corners(k):
+        accs = [jnp.zeros((8, 128), f32), jnp.zeros((8, 128), f32)]
+        for t in range(TILES):
+            for c in range(3):
+                base = 8 * (t % 16) + 2 * c
+                both = jnp.where(lane == 127, V[c, 0, rows(t)], V[c, PLANES - 1, rows(t)])
+                hit = jnp.logical_or(lane == base, lane == base + 1)
+                accs[t // 16] = jnp.where(hit, pltpu.roll(both, base + 1, 1), accs[t // 16])
+        for g in range(2):
+            CK[k, pl.ds(8 * g, 8)] = accs[g]
+
+    def corner_of(ref, k, t, c, by):
+        return pltpu.roll(ref[k, pl.ds(8 * (t // 16), 8)], (by - 8 * (t % 16) - 2 * c) % 128, 1)
+
     def trial(y, tiles):
-        back = lax.rem(128 - 2 * y, 128)
+        back = (128 - 2 * y) % 128 if isinstance(y, int) else lax.rem(128 - 2 * y, 128)
 
         def lower_dip(value, i, t):
-            halo = pltpu.roll(SG[i, rows(t)], back, 1)
+            halo = SG[i, rows(t)]
+            if not isinstance(back, int) or back:
+                halo = pltpu.roll(halo, back, 1)
             return value - jnp.where(lane == 0, halo, pltpu.roll(value, 1, 1))
 
         for t in tiles:
@@ -195,19 +233,22 @@
             V[1, y, r] = vy
             V[2, y, r] = vz
 
-    def stress(p, here, here_lead, over, over_lead, halo, halo_y, ghost=False, last=False):
+    def stress(p, here, here_lead, over, over_lead, halo, ghost=False, last=False, tiles=range(TILES)):
         def put(i, value):
-            if last:
+            if ghost:
+                S[i, p, r] = jnp.where(dn_y, value, S[i, p, r])
+            elif last:
                 str_out[S_ORDER[i], p - 1, r] = value
             else:
                 S[i, p, r] = value
 
-        for t in range(TILES - 1 if last else TILES):
+        for t in tiles:
+            if last and t == TILES - 1:
+                continue
             r = rows(t)
 
             def upper_dip(value, c):
-                edge_column = pltpu.roll(halo[r], 126 - 16 * c - 2 * halo_y, 1)
-                return jnp.where(lane == 127, edge_column, pltpu.roll(value, 127, 1)) - value
+                return jnp.where(lane == 127, halo(c, t), pltpu.roll(value, 127, 1)) - value
 
             vx, vy, vz = (here[here_lead(c) + (r,)] for c in range(3))
             ox, oy, oz = (over[over_lead(c) + (r,)] for c in range(3))
@@ -226,14 +267,20 @@
                     upper_dip(vx, 0) + (above(here, here_lead(2), t) - vz)
                 ))
 
-    def stress_own(k, y):
-        stress(y + 1, V, lambda c: (c, y), V, lambda c: (c, y + 1), UN, y, last=k == STEPS - 1)
+    def next_dip(y):
+        return lambda c, t: pltpu.roll(UN[rows(t)], 126 - 16 * c - 2 * y, 1)
+
+    def stress_own(k, tiles, y):
+        stress(
+            y + 1, V, lambda c: (c, y), V, lambda c: (c, y + 1), next_dip(y),
+            last=k == STEPS - 1, tiles=tiles,
+        )
 
     def stress_last(k):
-        stress(PLANES, V, lambda c: (c, PLANES - 1), VN, lambda c: (k, c), UN, PLANES - 1, last=k == STEPS - 1)
+        stress(PLANES, V, lambda c: (c, PLANES - 1), VN, lambda c: (k, c), next_dip(PLANES - 1), last=k == STEPS - 1)
 
     def stress_ghost(k):
-        stress(0, VP, lambda c: (k, c), V, lambda c: (c, 0), UD2, PLANES - 1, ghost=True)
+        stress(0, VP, lambda c: (k, c), V, lambda c: (c, 0), lambda c, t: corner_of(ZD2, k, t, c, 126), ghost=True)
 
     def column_ghost():
         for t in range(TILES):
@@ -249,19 +296,31 @@
                     )
                 return pltpu.roll(UM[pl.ds(8 * t + 1, 8)], (-16 * c) % 128, 1)
 
-            def next_strike(value, c):
-                corner = shifted(UD1, 14 - 16 * c)
-                return jnp.where(lane == 14, corner, pltpu.roll(value, 126, 1))
-
             vx, vy, vz = UM[r], shifted(UM, -16), shifted(UM, -32)
             ox, oy, oz = shifted(UO, -1), shifted(UO, -17), shifted(UO, -33)
             exx = upper_rows(0) - vx
-            eyy = next_strike(vy, 1) - vy
+            eyy = pltpu.roll(vy, 126, 1) - vy
             ezz = oz - vz
             c13, c44, c33 = CG[0, r], CG[1, r], CG[2, r]
-            SG[0, r] = SG[0, r] + DT * (c13 * (exx + eyy) + c33 * ezz)
+            zz = SG[0, r] + DT * (c13 * (exx + eyy) + c33 * ezz)
+            yz = SG[2, r] + DT * c44 * ((oy - vy) + (pltpu.roll(vz, 126, 1) - vz))
+            SG[0, r] = jnp.where(lane == 14, SG[0, r], zz)
             SG[1, r] = SG[1, r] + DT * c44 * ((ox - vx) + (upper_rows(2) - vz))
-            SG[2, r] = SG[2, r] + DT * c44 * ((oy - vy) + (next_strike(vz, 2) - vz))
+            SG[2, r] = jnp.where(lane == 14, SG[2, r], yz)
+            for i, value in enumerate((exx, vy, ezz, oy - vy, vz)):
+                GP[i, r] = value
+
+    def column_corner(k):
+        here = jnp.logical_and(lane == 14, dn_z)
+        for t in range(TILES):
+            r = rows(t)
+            exx, vy, ezz, oy_vy, vz = (GP[i, r] for i in range(5))
+            eyy = corner_of(ZD1, k, t, 1, 14) - vy
+            c13, c44, c33 = CG[0, r], CG[1, r], CG[2, r]
+            zz = SG[0, r] + DT * (c13 * (exx + eyy) + c33 * ezz)
+            yz = SG[2, r] + DT * c44 * (oy_vy + (corner_of(ZD1, k, t, 2, 14) - vz))
+            SG[0, r] = jnp.where(here, zz, SG[0, r])
+            SG[2, r] = jnp.where(here, yz, SG[2, r])
 
     def fault():
         for c in range(3):
@@ -323,10 +382,8 @@
         SG[...] = jnp.zeros(SG.shape, f32)
 
     ghost_rows = pl.ds(ROWS, 8)
-    every = pl.ds(1, PLANES)
     strike = pl.ds(YZ, 3)
     strike_c = pl.ds(C11, 4)
-    rest = pl.ds(C11, 5)
     for i in (YZ, YY, XY):
         loads["s7", i].wait()
     for i in range(6):
@@ -334,22 +391,37 @@
     loads["ve"].wait()
     for i in range(6):
         loads["ce", i].wait()
+    fields = [(SE, S, i, 1) for i in range(6)] + [(VE, V, i, 0) for i in range(3)]
+    fields += [(CE, C, i, 1) for i in range(6)]
+    for n, (src, _, i, _) in enumerate(fields):
+        for q in range(PLANES // 2):
+            first, second = src[i, 2 * q], src[i, 2 * q + 1]
+            low = jnp.where(is_minus, pltpu.roll(first, 4, 0), first)
+            high = jnp.where(is_minus, second, pltpu.roll(second, 4, 0))
+            XS[n, q] = jnp.where(sub < 4, low, high)
+
+    def spread(n):
+        _, dst, i, base = fields[n]
+        for q in range(PLANES // 2):
+            value = XR[n, q]
+            moved = pltpu.roll(value, 4, 0)
+            dst[i, base + 2 * q, ghost_rows] = jnp.where(is_minus, value, moved)
+            dst[i, base + 2 * q + 1, ghost_rows] = jnp.where(is_minus, moved, value)
+
+    for i in (ZZ, XZ, YZ, YY, XY, XX):
+        loads["s", i].wait()
+    accs = pack(S, ZZ, 1, PI.at[0], 16)
+    PI[0, pl.ds(64, 8)] = jnp.where(is_minus, pltpu.roll(accs[7], 64, 1), accs[0])
     pl.semaphore_wait(barrier, count)
     message("y0", S.at[strike, PLANES, own], S.at[strike, 0, own], 0, 1, 0)
     message("xy0", SE.at[strike, PLANES - 1], S.at[strike, 0, ghost_rows], 1, 1, 0)
-    message("x0", SE, S.at[:, every, ghost_rows], 1, 0, 0)
-    message("xv", VE, V.at[:, :, ghost_rows], 1, 0, 0)
-    message("xb", CE.at[BUO], C.at[BUO, every, ghost_rows], 1, 0, 0)
-    for i in (ZZ, XZ, YZ, YY, XY, XX):
-        loads["s", i].wait()
-    accs = pack(S, ZZ, 1, PI.at[0], 16)
+    message("xa", XS.at[pl.ds(0, 10)], XR.at[pl.ds(0, 10)], 1, 0, 0)
     message("z0", PI.at[0, pl.ds(0, 64)], ZI.at[0, pl.ds(0, 64)], 0, 0, 1)
-    PI[0, pl.ds(64, 8)] = jnp.where(is_minus, pltpu.roll(accs[7], 64, 1), accs[0])
     message("xz0", PI.at[0, pl.ds(64, 8)], ZI.at[0, pl.ds(64, 8)], 1, 0, 1)
     loads["v"].wait()
     for i in range(6):
         loads[i].wait()
-    message("xc", CE.at[rest], C.at[rest, every, ghost_rows], 1, 0, 0)
+    message("xc", XS.at[pl.ds(10, 5)], XR.at[pl.ds(10, 5)], 1, 0, 0)
     message("yc", C.at[strike_c, PLANES, own], C.at[strike_c, 0, own], 0, 1, 0)
     message("xyc", CE.at[strike_c, PLANES - 1], C.at[strike_c, 0, ghost_rows], 1, 1, 0)
     accs = pack(C, C13, 1, PI.at[1], 16)
@@ -392,20 +464,33 @@
         lax.fori_loop(first, last, step, 0)
 
     planes(1, PLANES, lambda y: trial(y, own_tiles))
-    arrived("x0")
-    arrived("xv")
-    arrived("xb")
+
+    def columns_early(k):
+        pack(V, 0, 0, PK.at[k, 0], TILES, early)
+        message(("zb1", k), PK.at[k, 0], ZN.at[k, 0], 0, 0, -1)
+        if k < STEPS - 1:
+            message(("zf1", k), PK.at[k, 0], ZM.at[k, 0], 0, 0, 1)
+
+    columns_early(0)
+    arrived("xa")
+    for n in range(10):
+        spread(n)
     arrived("xy0")
     for y in range(PLANES):
         FB[6, pl.ds(y, 1)] = C[BUO, y + 1, pl.ds(own_f, 1)]
         FB[7, pl.ds(y, 1)] = C[BUO, y + 1, pl.ds(other_f, 1)]
-    planes(0, PLANES, lambda y: trial(y, [TILES - 1]))
+    for y in range(PLANES):
+        trial(y, [TILES - 1])
     arrived("y0")
     planes(0, 1, lambda y: trial(y, own_tiles))
 
     for k in range(STEPS):
         last = k == STEPS - 1
         fault()
+        if not last:
+            corners(k)
+            message(("d1", k), CK.at[k], ZD1.at[k], 0, -1, 1)
+            message(("d2", k), CK.at[k], ZD2.at[k], 0, 1, -1)
         message(("yb", k), V.at[:, 0], VN.at[k], 0, -1, 0)
         if not last:
             message(("yf", k), V.at[:, PLANES - 1], VP.at[k], 0, 1, 0)
@@ -417,12 +502,10 @@
                     vel_out[c, y] = V[c, y, own]
 
             planes(0, PLANES, copy_plane)
-        pack(V, 0, 0, PK.at[k], TILES)
-        message(("zb", k), PK.at[k], ZN.at[k], 0, 0, -1)
+        pack(V, 0, 0, PK.at[k, 1], TILES, lambda y, t: not early(y, t))
+        message(("zb", k), PK.at[k, 1], ZN.at[k, 1], 0, 0, -1)
         if not last:
-            message(("zf", k), PK.at[k], ZM.at[k], 0, 0, 1)
-            message(("d1", k), PK.at[k], ZD1.at[k], 0, -1, 1)
-            message(("d2", k), PK.at[k], ZD2.at[k], 0, 1, -1)
+            message(("zf", k), PK.at[k, 1], ZM.at[k, 1], 0, 0, 1)
         if k == 0:
             arrived("zc")
             arrived("xzc")
@@ -432,44 +515,60 @@
                 columns(ZI.at[1], CG)
 
             arrived("xc")
+            for n in range(10, 15):
+                spread(n)
             gone("y0")
+        arrived(("zb1", k))
+        unpack(ZN.at[k, 0], UN)
+        planes(1, PLANES - 1, functools.partial(stress_own, k, INNER))
         arrived(("zb", k))
-        unpack(ZN.at[k], UN)
-        planes(0, PLANES - 1, functools.partial(stress_own, k))
+        merge(ZN.at[k], UN)
+        for y in range(1, PLANES - 1):
+            stress_own(k, FAULT, y)
+        stress_own(k, all_tiles, 0)
         if last:
             arrived(("yb", k))
-            planes(0, 1, lambda y: stress_last(k))
+            stress_last(k)
             break
+        arrived(("zf1", k))
         arrived(("zf", k))
-        arrived(("d1", k))
 
         @pl.when(dn_z)
         def _():
-            unpack(ZM.at[k], UM)
-            unpack(ZD1.at[k], UD1)
-            unpack(PK.at[k], UO)
+            merge(ZM.at[k], UM)
+            merge(PK.at[k], UO)
             column_ghost()
 
         planes(1, PLANES - 1, lambda y: trial(y, all_tiles))
+        columns_early(k + 1)
         if k == 0:
             arrived("yc")
             arrived("xyc")
+        arrived(("d1", k))
         arrived(("d2", k))
-        arrived(("yf", k))
-
-        @pl.when(dn_y)
-        def _():
-            unpack(ZD2.at[k], UD2)
-            stress_ghost(k)
-
-        arrived(("yb", k))
         gone(("yb", k))
         gone(("yf", k))
-        planes(0, 1, lambda y: stress_last(k))
-        planes(0, 2, lambda i: trial((PLANES - 1) * i, all_tiles))
+        arrived(("yf", k))
+        arrived(("yb", k))
+        column_corner(k)
+        stress_ghost(k)
+        stress_last(k)
+        trial(0, all_tiles)
+        trial(PLANES - 1, all_tiles)
 
     for name in list(sent):
         gone(name)
+
+
+def writer(vel_in, str_in, slip_in, vel_out, str_out, slip_out, sem):
+    pairs = [(slip_in, slip_out)]
+    pairs += [(str_in.at[i], str_out.at[i]) for i in range(6)]
+    pairs += [(vel_in.at[i], vel_out.at[i]) for i in range(3)]
+    copies = [pltpu.make_async_copy(src, dst, sem.at[i]) for i, (src, dst) in enumerate(pairs)]
+    for copy in copies:
+        copy.start()
+    for copy in copies:
+        copy.wait()
 
 
 def local(
@@ -482,6 +581,7 @@
     tile = pltpu.VMEM((8, 128), f32)
     plane = (EXT, 128)
     packed = (72, 128)
+    corner = (16, 128)
     large = [
         pltpu.with_memory_space_constraint(x, pltpu.HBM)
         for x in (
@@ -489,7 +589,7 @@
             prestress, fault_mask, region_ids, inverse_rate, slip_prev, region_a, region_normal,
         )
     ]
-    return pl.pallas_call(
+    results = pl.pallas_call(
         kernel,
         out_shape=(
             jax.ShapeDtypeStruct(velocity.shape, f32),
@@ -504,15 +604,15 @@
             pltpu.VMEM((6, PLANES + 1) + plane, f32),
             pltpu.VMEM((STEPS, 3) + plane, f32),
             pltpu.VMEM((STEPS - 1, 3) + plane, f32),
-            pltpu.VMEM((STEPS,) + packed, f32),
-            pltpu.VMEM((STEPS,) + packed, f32),
-            pltpu.VMEM((STEPS - 1,) + packed, f32),
-            pltpu.VMEM((STEPS - 1,) + packed, f32),
-            pltpu.VMEM((STEPS - 1,) + packed, f32),
+            pltpu.VMEM((STEPS, 2) + packed, f32),
+            pltpu.VMEM((STEPS, 2) + packed, f32),
+            pltpu.VMEM((STEPS - 1, 2) + packed, f32),
+            pltpu.VMEM((5,) + plane, f32),
+            pltpu.VMEM((STEPS - 1,) + corner, f32),
+            pltpu.VMEM((STEPS - 1,) + corner, f32),
+            pltpu.VMEM((STEPS - 1,) + corner, f32),
             pltpu.VMEM((2,) + packed, f32),
             pltpu.VMEM((2,) + packed, f32),
-            pltpu.VMEM(plane, f32),
-            pltpu.VMEM(plane, f32),
             pltpu.VMEM(plane, f32),
             pltpu.VMEM(plane, f32),
             pltpu.VMEM(plane, f32),
@@ -522,6 +622,8 @@
             pltpu.VMEM((6, PLANES, 8, 128), f32),
             pltpu.VMEM((3, PLANES, 8, 128), f32),
             pltpu.VMEM((6, PLANES, 8, 128), f32),
+            pltpu.VMEM((15, PLANES // 2, 8, 128), f32),
+            pltpu.VMEM((15, PLANES // 2, 8, 128), f32),
             pltpu.VMEM((2, 8, 128), f32),
             pltpu.VMEM((8, 128), jnp.int32),
             pltpu.VMEM((8, 128), jnp.int32),
@@ -531,14 +633,23 @@
             pltpu.SMEM((8,), f32),
             pltpu.SMEM((8,), f32),
             pltpu.SemaphoreType.DMA((40,)),
-            pltpu.SemaphoreType.DMA((32,)),
-            pltpu.SemaphoreType.DMA((32,)),
+            pltpu.SemaphoreType.DMA((40,)),
+            pltpu.SemaphoreType.DMA((40,)),
         ],
         compiler_params=pltpu.CompilerParams(
             collective_id=0, has_side_effects=True, vmem_limit_bytes=40 * 1024 * 1024
         ),
         name="rupture",
     )(*large)
+    return pl.pallas_call(
+        writer,
+        out_shape=tuple(jax.ShapeDtypeStruct(x.shape, f32) for x in results),
+        in_specs=[vmem] * 3,
+        out_specs=(hbm, hbm, hbm),
+        scratch_shapes=[pltpu.SemaphoreType.DMA((16,))],
+        compiler_params=pltpu.CompilerParams(vmem_limit_bytes=1024 * 1024),
+        name="writer",
+    )(*results)
 
 
 def solution(mesh):

time: 45.8 us -> 35.2 us (0.77)
  Pallas kernels: 41.1 us -> 34.3 us
  local copies, waits for them, and re-layouts: 3.4 us -> 0 us
    pallas_call x1, Pallas kernels: 41.1 us -> 32 us  [local(): pl.pallas_call(kernel, out_shape=(jax.ShapeDtypeStruct(velocity.shape, f3...]
    unnamed x3 -> x0, local copies, waits for them, and re-layouts: 3.4 us -> none
    pallas_call x0 -> x1, Pallas kernels: none -> 2.32 us  [local(): pl.pallas_call(writer, out_shape=tuple((jax.ShapeDtypeStruct(x.shape, f32...]
where the time goes in v2:
time: 35.2 us; the launch traced here: 35 us
  Pallas kernels  34.3 us (97%)
  between operations  0.64 us (2%)
    pallas_call x1, Pallas kernels, local(): pl.pallas_call(kernel, out_shape=(jax.ShapeDtypeStruct(velocity.shape, f3...  32 us
    pallas_call x1, Pallas kernels, local(): pl.pallas_call(writer, out_shape=tuple((jax.ShapeDtypeStruct(x.shape, f32...  2.32 us

profile of v2, /device:TPU:1, one launch (start us, length us, event | category | flops | bytes accessed | tf_op | source)
XLA Modules:
  0.0 35.0 jit_solution(14099389054748264480)
XLA Ops:
  0.6 32.0 %rupture.1 = (f32[3,8,128,128]{3,2,1,0:T(8,128)S(1)}, f32[6,8,128,128]{3,2,1,0:T(8,128)S(1)}, f32[8,128]{1,0:T(8,128)S(1)}) custom-call(f32[3,8,128,128]{3,2,1,0:T(8,128)} %vel_hbm.1, f32[6,8,128,128]{3,2,1,0:T(8,128)} %str_hbm.1, f32[8,128,128]{2,1,0:T(8,128)} %buo_hbm.1, f32[8,128,128]{2,1,0:T(8,128)} %c11_hbm.1, f32[8,128,128]{2,1,0:T(8,128)} %c13_hbm.1, ...), custom_call_target="tpu_custom_call" | custom-call | tf_op jit(solution)/shard_map/rupture/pallas_call | solution.py:592
  32.7 2.3 %writer.1 = (f32[3,8,128,128]{3,2,1,0:T(8,128)}, f32[6,8,128,128]{3,2,1,0:T(8,128)}, f32[8,128]{1,0:T(8,128)}) custom-call(f32[3,8,128,128]{3,2,1,0:T(8,128)S(1)} %get-tuple-element.6.vel_in, f32[6,8,128,128]{3,2,1,0:T(8,128)S(1)} %get-tuple-element.7.str_in, f32[8,128]{1,0:T(8,128)S(1)} %get-tuple-element.8.slip_in), custom_call_target="tpu_custom_call" | custom-call | tf_op jit(solution)/shard_map/writer/pallas_call | solution.py:644

commit v3 on v2

--- a/solution.py
+++ b/solution.py
@@ -20,7 +20,26 @@
 ROWS = 128
 TILES = 17
 EXT = 8 * TILES
-GHOST = slice(ROWS, EXT)
+
+LOW, HIGH = 3, 13
+
+
+def part_tiles(k, part):
+    if part == 0:
+        return [*range(LOW - k), *range(HIGH + k, TILES)]
+    return [*range(LOW - k, HIGH + k)]
+
+
+def part_rows(k, part):
+    if part == 0:
+        return [(0, 8 * (LOW - k)), (8 * (HIGH + k), EXT)]
+    return [(8 * (LOW - k), 8 * (HIGH + k))]
+
+
+def ghost_tiles(k, part):
+    if part == 0:
+        return [*range(LOW - k - 1), *range(HIGH + k, TILES)]
+    return [*range(LOW - k - 1, HIGH + k)]
 
 
 def kernel(
@@ -148,19 +167,17 @@
             return jnp.where(sub == 7, 0.0, pltpu.roll(ref[lead + (rows(t),)], 7, 0))
         return ref[lead + (pl.ds(8 * t + 1, 8),)]
 
-    def pack(ref, lead, plane0, out, tiles, pick=lambda y, t: True):
-        groups = (tiles + 1) // 2
+    def pack(ref, lead, plane0, out, tiles):
+        groups = (len(tiles) + 1) // 2
 
         def body(c, accs):
             accs = list(accs)
             for y in range(PLANES):
-                for t in range(tiles):
-                    if not pick(y, t):
-                        continue
-                    base = 64 * (t % 2) + 16 * c + 2 * y
+                for j, t in enumerate(tiles):
+                    base = 64 * (j % 2) + 16 * c + 2 * y
                     moved = pltpu.roll(ref[lead + c, plane0 + y, rows(t)], base + 1, 1)
                     hit = jnp.logical_or(lane == base, lane == base + 1)
-                    accs[t // 2] = jnp.where(hit, moved, accs[t // 2])
+                    accs[j // 2] = jnp.where(hit, moved, accs[j // 2])
             return tuple(accs)
 
         accs = lax.fori_loop(0, 3, body, tuple(jnp.zeros((8, 128), f32) for _ in range(groups)))
@@ -168,44 +185,25 @@
             out[pl.ds(8 * g, 8)] = accs[g]
         return accs
 
-    FAULT = (0, TILES - 2, TILES - 1)
-    INNER = range(1, TILES - 2)
-
-    def early(y, t):
-        return 0 < y < PLANES - 1 and t in INNER
-
-    def merge(src, dst):
-        strike_index = lax.rem(lane, 16) // 2
-        outer = jnp.logical_or(strike_index == 0, strike_index == PLANES - 1)
-        for g in range((TILES + 1) // 2):
-            late = outer
-            if 2 * g in FAULT:
-                late = jnp.logical_or(late, lane < 64)
-            if 2 * g + 1 in FAULT:
-                late = jnp.logical_or(late, lane >= 64)
-            tile = jnp.where(late, src[1, pl.ds(8 * g, 8)], src[0, pl.ds(8 * g, 8)])
-            dst[rows(2 * g)] = tile
-            if 2 * g + 1 < TILES:
-                dst[rows(2 * g + 1)] = pltpu.roll(tile, 64, 1)
-
-    def unpack(src, dst):
-        for t in range(TILES):
-            tile = src[pl.ds(8 * (t // 2), 8)]
-            dst[rows(t)] = tile if t % 2 == 0 else pltpu.roll(tile, 64, 1)
-
-    def corners(k):
-        accs = [jnp.zeros((8, 128), f32), jnp.zeros((8, 128), f32)]
-        for t in range(TILES):
+    def unpack(src, dst, tiles):
+        for j, t in enumerate(tiles):
+            tile = src[pl.ds(8 * (j // 2), 8)]
+            dst[rows(t)] = tile if j % 2 == 0 else pltpu.roll(tile, 64, 1)
+
+    def corners(k, part):
+        acc = jnp.zeros((8, 128), f32)
+        for j, t in enumerate(part_tiles(k, part)):
             for c in range(3):
-                base = 8 * (t % 16) + 2 * c
+                base = 8 * j + 2 * c
                 both = jnp.where(lane == 127, V[c, 0, rows(t)], V[c, PLANES - 1, rows(t)])
                 hit = jnp.logical_or(lane == base, lane == base + 1)
-                accs[t // 16] = jnp.where(hit, pltpu.roll(both, base + 1, 1), accs[t // 16])
-        for g in range(2):
-            CK[k, pl.ds(8 * g, 8)] = accs[g]
+                acc = jnp.where(hit, pltpu.roll(both, base + 1, 1), acc)
+        CK[k, part] = acc
 
     def corner_of(ref, k, t, c, by):
-        return pltpu.roll(ref[k, pl.ds(8 * (t // 16), 8)], (by - 8 * (t % 16) - 2 * c) % 128, 1)
+        part = 0 if t in part_tiles(k, 0) else 1
+        j = part_tiles(k, part).index(t)
+        return pltpu.roll(ref[k, part], (by - 8 * j - 2 * c) % 128, 1)
 
     def trial(y, tiles):
         back = (128 - 2 * y) % 128 if isinstance(y, int) else lax.rem(128 - 2 * y, 128)
@@ -276,14 +274,14 @@
             last=k == STEPS - 1, tiles=tiles,
         )
 
-    def stress_last(k):
-        stress(PLANES, V, lambda c: (c, PLANES - 1), VN, lambda c: (k, c), next_dip(PLANES - 1), last=k == STEPS - 1)
-
-    def stress_ghost(k):
-        stress(0, VP, lambda c: (k, c), V, lambda c: (c, 0), lambda c, t: corner_of(ZD2, k, t, c, 126), ghost=True)
-
-    def column_ghost():
-        for t in range(TILES):
+    def stress_last(k, tiles):
+        stress(PLANES, V, lambda c: (c, PLANES - 1), VN, lambda c: (k, c), next_dip(PLANES - 1), last=k == STEPS - 1, tiles=tiles)
+
+    def stress_ghost(k, tiles):
+        stress(0, VP, lambda c: (k, c), V, lambda c: (c, 0), lambda c, t: corner_of(ZD2, k, t, c, 126), ghost=True, tiles=tiles)
+
+    def column_ghost(tiles):
+        for t in tiles:
             r = rows(t)
 
             def shifted(ref, by):
@@ -310,9 +308,9 @@
             for i, value in enumerate((exx, vy, ezz, oy - vy, vz)):
                 GP[i, r] = value
 
-    def column_corner(k):
+    def column_corner(k, tiles):
         here = jnp.logical_and(lane == 14, dn_z)
-        for t in range(TILES):
+        for t in tiles:
             r = rows(t)
             exx, vy, ezz, oy_vy, vz = (GP[i, r] for i in range(5))
             eyy = corner_of(ZD1, k, t, 1, 14) - vy
@@ -410,11 +408,16 @@
 
     for i in (ZZ, XZ, YZ, YY, XY, XX):
         loads["s", i].wait()
-    accs = pack(S, ZZ, 1, PI.at[0], 16)
+    accs = pack(S, ZZ, 1, PI.at[0], range(16))
     PI[0, pl.ds(64, 8)] = jnp.where(is_minus, pltpu.roll(accs[7], 64, 1), accs[0])
     pl.semaphore_wait(barrier, count)
-    message("y0", S.at[strike, PLANES, own], S.at[strike, 0, own], 0, 1, 0)
+    first_rows = [(0, 8 * LOW), (8 * HIGH, ROWS), (8 * LOW, 8 * HIGH)]
+    for i, (top, end) in enumerate(first_rows[:2]):
+        some = pl.ds(top, end - top)
+        message(("y0", i), S.at[strike, PLANES, some], S.at[strike, 0, some], 0, 1, 0)
     message("xy0", SE.at[strike, PLANES - 1], S.at[strike, 0, ghost_rows], 1, 1, 0)
+    mid = pl.ds(8 * LOW, 8 * (HIGH - LOW))
+    message(("y0", 2), S.at[strike, PLANES, mid], S.at[strike, 0, mid], 0, 1, 0)
     message("xa", XS.at[pl.ds(0, 10)], XR.at[pl.ds(0, 10)], 1, 0, 0)
     message("z0", PI.at[0, pl.ds(0, 64)], ZI.at[0, pl.ds(0, 64)], 0, 0, 1)
     message("xz0", PI.at[0, pl.ds(64, 8)], ZI.at[0, pl.ds(64, 8)], 1, 0, 1)
@@ -424,7 +427,7 @@
     message("xc", XS.at[pl.ds(10, 5)], XR.at[pl.ds(10, 5)], 1, 0, 0)
     message("yc", C.at[strike_c, PLANES, own], C.at[strike_c, 0, own], 0, 1, 0)
     message("xyc", CE.at[strike_c, PLANES - 1], C.at[strike_c, 0, ghost_rows], 1, 1, 0)
-    accs = pack(C, C13, 1, PI.at[1], 16)
+    accs = pack(C, C13, 1, PI.at[1], range(16))
     message("zc", PI.at[1, pl.ds(0, 64)], ZI.at[1, pl.ds(0, 64)], 0, 0, 1)
     PI[1, pl.ds(64, 8)] = jnp.where(is_minus, pltpu.roll(accs[7], 64, 1), accs[0])
     message("xzc", PI.at[1, pl.ds(64, 8)], ZI.at[1, pl.ds(64, 8)], 1, 0, 1)
@@ -465,96 +468,137 @@
 
     planes(1, PLANES, lambda y: trial(y, own_tiles))
 
-    def columns_early(k):
-        pack(V, 0, 0, PK.at[k, 0], TILES, early)
-        message(("zb1", k), PK.at[k, 0], ZN.at[k, 0], 0, 0, -1)
+    def send_strike(k, part):
         if k < STEPS - 1:
-            message(("zf1", k), PK.at[k, 0], ZM.at[k, 0], 0, 0, 1)
-
-    columns_early(0)
+            corners(k, part)
+            message(("d1", k, part), CK.at[k, part], ZD1.at[k, part], 0, -1, 1)
+            message(("d2", k, part), CK.at[k, part], ZD2.at[k, part], 0, 1, -1)
+        for i, (top, end) in enumerate(part_rows(k, part)):
+            some = pl.ds(top, end - top)
+            message(("yb", k, part, i), V.at[:, 0, some], VN.at[k, :, some], 0, -1, 0)
+            if k < STEPS - 1:
+                message(("yf", k, part, i), V.at[:, PLANES - 1, some], VP.at[k, :, some], 0, 1, 0)
+
+    def send_dip(k, part):
+        tiles = part_tiles(k, part)
+        size = pl.ds(0, 8 * ((len(tiles) + 1) // 2))
+        pack(V, 0, 0, PK.at[k, part], tiles)
+        message(("zb", k, part), PK.at[k, part, size], ZN.at[k, part, size], 0, 0, -1)
+        if k < STEPS - 1:
+            message(("zf", k, part), PK.at[k, part, size], ZM.at[k, part, size], 0, 0, 1)
+
+    def interior(k, part):
+        tiles = part_tiles(k, part)
+        arrived(("zb", k, part))
+        unpack(ZN.at[k, part], UN, tiles)
+        if part == 0:
+            for y in range(PLANES - 1):
+                stress_own(k, tiles, y)
+        else:
+            stress_own(k, tiles, 0)
+
+            def two(i):
+                stress_own(k, tiles, 2 * i + 1)
+                stress_own(k, tiles, 2 * i + 2)
+
+            planes(0, PLANES // 2 - 1, two)
+        if k == STEPS - 1:
+            return
+        arrived(("zf", k, part))
+
+        @pl.when(dn_z)
+        def _():
+            unpack(ZM.at[k, part], UM, tiles)
+            unpack(PK.at[k, part], UO, tiles)
+            column_ghost(ghost_tiles(k, part))
+
+        after = part_tiles(k + 1, part)
+        if part == 0:
+            for y in range(1, PLANES - 1):
+                trial(y, after)
+        else:
+
+            def two_trials(i):
+                trial(2 * i + 1, after)
+                trial(2 * i + 2, after)
+
+            planes(0, PLANES // 2 - 1, two_trials)
+
+    def boundary(k, part):
+        if k == 0 and part == 0:
+            arrived("yc")
+            arrived("xyc")
+        for name in ("d1", "d2"):
+            arrived((name, k, part))
+        for i in range(len(part_rows(k, part))):
+            for name in ("yf", "yb"):
+                gone((name, k, part, i))
+                arrived((name, k, part, i))
+        column_corner(k, ghost_tiles(k, part))
+        stress_ghost(k, ghost_tiles(k, part))
+        stress_last(k, part_tiles(k, part))
+        after = part_tiles(k + 1, part)
+        trial(0, after)
+        trial(PLANES - 1, after)
+
     arrived("xa")
     for n in range(10):
         spread(n)
-    arrived("xy0")
     for y in range(PLANES):
         FB[6, pl.ds(y, 1)] = C[BUO, y + 1, pl.ds(own_f, 1)]
         FB[7, pl.ds(y, 1)] = C[BUO, y + 1, pl.ds(other_f, 1)]
-    for y in range(PLANES):
+    for y in range(1, PLANES):
         trial(y, [TILES - 1])
-    arrived("y0")
-    planes(0, 1, lambda y: trial(y, own_tiles))
-
-    for k in range(STEPS):
-        last = k == STEPS - 1
+    arrived("xy0")
+    arrived(("y0", 0))
+    arrived(("y0", 1))
+    trial(0, part_tiles(0, 0))
+    fault()
+    send_strike(0, 0)
+    send_dip(0, 0)
+    arrived(("y0", 2))
+    trial(0, part_tiles(0, 1))
+    send_strike(0, 1)
+    send_dip(0, 1)
+
+    arrived("zc")
+    arrived("xzc")
+
+    @pl.when(dn_z)
+    def _():
+        columns(ZI.at[1], CG)
+
+    arrived("xc")
+    for n in range(10, 15):
+        spread(n)
+    for i in range(3):
+        gone(("y0", i))
+
+    for k in range(STEPS - 1):
+        interior(k, 0)
+        boundary(k, 0)
         fault()
-        if not last:
-            corners(k)
-            message(("d1", k), CK.at[k], ZD1.at[k], 0, -1, 1)
-            message(("d2", k), CK.at[k], ZD2.at[k], 0, 1, -1)
-        message(("yb", k), V.at[:, 0], VN.at[k], 0, -1, 0)
-        if not last:
-            message(("yf", k), V.at[:, PLANES - 1], VP.at[k], 0, 1, 0)
-        else:
-            slip_out[...] = slip[...]
-
-            def copy_plane(y):
-                for c in range(3):
-                    vel_out[c, y] = V[c, y, own]
-
-            planes(0, PLANES, copy_plane)
-        pack(V, 0, 0, PK.at[k, 1], TILES, lambda y, t: not early(y, t))
-        message(("zb", k), PK.at[k, 1], ZN.at[k, 1], 0, 0, -1)
-        if not last:
-            message(("zf", k), PK.at[k, 1], ZM.at[k, 1], 0, 0, 1)
-        if k == 0:
-            arrived("zc")
-            arrived("xzc")
-
-            @pl.when(dn_z)
-            def _():
-                columns(ZI.at[1], CG)
-
-            arrived("xc")
-            for n in range(10, 15):
-                spread(n)
-            gone("y0")
-        arrived(("zb1", k))
-        unpack(ZN.at[k, 0], UN)
-        planes(1, PLANES - 1, functools.partial(stress_own, k, INNER))
-        arrived(("zb", k))
-        merge(ZN.at[k], UN)
-        for y in range(1, PLANES - 1):
-            stress_own(k, FAULT, y)
-        stress_own(k, all_tiles, 0)
-        if last:
-            arrived(("yb", k))
-            stress_last(k)
-            break
-        arrived(("zf1", k))
-        arrived(("zf", k))
-
-        @pl.when(dn_z)
-        def _():
-            merge(ZM.at[k], UM)
-            merge(PK.at[k], UO)
-            column_ghost()
-
-        planes(1, PLANES - 1, lambda y: trial(y, all_tiles))
-        columns_early(k + 1)
-        if k == 0:
-            arrived("yc")
-            arrived("xyc")
-        arrived(("d1", k))
-        arrived(("d2", k))
-        gone(("yb", k))
-        gone(("yf", k))
-        arrived(("yf", k))
-        arrived(("yb", k))
-        column_corner(k)
-        stress_ghost(k)
-        stress_last(k)
-        trial(0, all_tiles)
-        trial(PLANES - 1, all_tiles)
+        send_strike(k + 1, 0)
+        send_dip(k + 1, 0)
+        interior(k, 1)
+        boundary(k, 1)
+        send_strike(k + 1, 1)
+        send_dip(k + 1, 1)
+
+    k = STEPS - 1
+    slip_out[...] = slip[...]
+
+    def copy_plane(y):
+        for c in range(3):
+            vel_out[c, y] = V[c, y, own]
+
+    planes(0, PLANES, copy_plane)
+    for part in range(2):
+        interior(k, part)
+    for part in range(2):
+        for i in range(len(part_rows(k, part))):
+            arrived(("yb", k, part, i))
+        stress_last(k, part_tiles(k, part))
 
     for name in list(sent):
         gone(name)
@@ -581,7 +625,8 @@
     tile = pltpu.VMEM((8, 128), f32)
     plane = (EXT, 128)
     packed = (72, 128)
-    corner = (16, 128)
+    half = (56, 128)
+    corner = (2, 8, 128)
     large = [
         pltpu.with_memory_space_constraint(x, pltpu.HBM)
         for x in (
@@ -604,9 +649,9 @@
             pltpu.VMEM((6, PLANES + 1) + plane, f32),
             pltpu.VMEM((STEPS, 3) + plane, f32),
             pltpu.VMEM((STEPS - 1, 3) + plane, f32),
-            pltpu.VMEM((STEPS, 2) + packed, f32),
-            pltpu.VMEM((STEPS, 2) + packed, f32),
-            pltpu.VMEM((STEPS - 1, 2) + packed, f32),
+            pltpu.VMEM((STEPS, 2) + half, f32),
+            pltpu.VMEM((STEPS, 2) + half, f32),
+            pltpu.VMEM((STEPS - 1, 2) + half, f32),
             pltpu.VMEM((5,) + plane, f32),
             pltpu.VMEM((STEPS - 1,) + corner, f32),
             pltpu.VMEM((STEPS - 1,) + corner, f32),
@@ -633,8 +678,8 @@
             pltpu.SMEM((8,), f32),
             pltpu.SMEM((8,), f32),
             pltpu.SemaphoreType.DMA((40,)),
-            pltpu.SemaphoreType.DMA((40,)),
-            pltpu.SemaphoreType.DMA((40,)),
+            pltpu.SemaphoreType.DMA((64,)),
+            pltpu.SemaphoreType.DMA((64,)),
         ],
         compiler_params=pltpu.CompilerParams(
             collective_id=0, has_side_effects=True, vmem_limit_bytes=40 * 1024 * 1024

time: 35.2 us -> 36.9 us (1.048)
  Pallas kernels: 34.3 us -> 36.1 us
    pallas_call x1, Pallas kernels: 32 us -> 33.8 us  [local(): pl.pallas_call(kernel, out_shape=(jax.ShapeDtypeStruct(velocity.shape, f3...]
where the time goes in v3:
time: 36.9 us; the launch traced here: 36.8 us
  Pallas kernels  36.1 us (98%)
  between operations  0.64 us (2%)
    pallas_call x1, Pallas kernels, local(): pl.pallas_call(kernel, out_shape=(jax.ShapeDtypeStruct(velocity.shape, f3...  33.8 us
    pallas_call x1, Pallas kernels, local(): pl.pallas_call(writer, out_shape=tuple((jax.ShapeDtypeStruct(x.shape, f32...  2.32 us

profile of v3, /device:TPU:1, one launch (start us, length us, event | category | flops | bytes accessed | tf_op | source)
XLA Modules:
  0.0 36.8 jit_solution(3979596056995251697)
XLA Ops:
  0.6 33.8 %rupture.1 = (f32[3,8,128,128]{3,2,1,0:T(8,128)S(1)}, f32[6,8,128,128]{3,2,1,0:T(8,128)S(1)}, f32[8,128]{1,0:T(8,128)S(1)}) custom-call(f32[3,8,128,128]{3,2,1,0:T(8,128)} %vel_hbm.1, f32[6,8,128,128]{3,2,1,0:T(8,128)} %str_hbm.1, f32[8,128,128]{2,1,0:T(8,128)} %buo_hbm.1, f32[8,128,128]{2,1,0:T(8,128)} %c11_hbm.1, f32[8,128,128]{2,1,0:T(8,128)} %c13_hbm.1, ...), custom_call_target="tpu_custom_call" | custom-call | tf_op jit(solution)/shard_map/rupture/pallas_call | solution.py:637
  34.5 2.3 %writer.1 = (f32[3,8,128,128]{3,2,1,0:T(8,128)}, f32[6,8,128,128]{3,2,1,0:T(8,128)}, f32[8,128]{1,0:T(8,128)}) custom-call(f32[3,8,128,128]{3,2,1,0:T(8,128)S(1)} %get-tuple-element.6.vel_in, f32[6,8,128,128]{3,2,1,0:T(8,128)S(1)} %get-tuple-element.7.str_in, f32[8,128]{1,0:T(8,128)S(1)} %get-tuple-element.8.slip_in), custom_call_target="tpu_custom_call" | custom-call | tf_op jit(solution)/shard_map/writer/pallas_call | solution.py:689

commit v4 on v2

--- a/solution.py
+++ b/solution.py
@@ -282,9 +282,18 @@
     def stress_ghost(k):
         stress(0, VP, lambda c: (k, c), V, lambda c: (c, 0), lambda c, t: corner_of(ZD2, k, t, c, 126), ghost=True)
 
-    def column_ghost():
-        for t in range(TILES):
+    def column_ghost(early):
+        in_time = jnp.logical_and(lane >= 2, lane < 12)
+        for t in range(1, TILES - 3) if early else range(TILES):
             r = rows(t)
+
+            def put(i, value, corner):
+                skip = lane == 14 if corner else None
+                if early:
+                    skip = jnp.logical_not(in_time)
+                elif 1 <= t < TILES - 3:
+                    skip = jnp.logical_or(in_time, skip) if corner else in_time
+                SG[i, r] = value if skip is None else jnp.where(skip, SG[i, r], value)
 
             def shifted(ref, by):
                 return pltpu.roll(ref[r], by % 128, 1)
@@ -304,9 +313,12 @@
             c13, c44, c33 = CG[0, r], CG[1, r], CG[2, r]
             zz = SG[0, r] + DT * (c13 * (exx + eyy) + c33 * ezz)
             yz = SG[2, r] + DT * c44 * ((oy - vy) + (pltpu.roll(vz, 126, 1) - vz))
-            SG[0, r] = jnp.where(lane == 14, SG[0, r], zz)
-            SG[1, r] = SG[1, r] + DT * c44 * ((ox - vx) + (upper_rows(2) - vz))
-            SG[2, r] = jnp.where(lane == 14, SG[2, r], yz)
+            xz = SG[1, r] + DT * c44 * ((ox - vx) + (upper_rows(2) - vz))
+            put(0, zz, True)
+            put(1, xz, False)
+            put(2, yz, True)
+            if early:
+                continue
             for i, value in enumerate((exx, vy, ezz, oy - vy, vz)):
                 GP[i, r] = value
 
@@ -484,28 +496,36 @@
     arrived("y0")
     planes(0, 1, lambda y: trial(y, own_tiles))
 
+    pieces = [(8, 40), (0, 8), (40, EXT)]
+
+    def send_strike(k, chosen):
+        for i in chosen:
+            some = pl.ds(pieces[i][0], pieces[i][1] - pieces[i][0])
+            message(("yb", k, i), V.at[:, 0, some], VN.at[k, :, some], 0, -1, 0)
+            if k < STEPS - 1:
+                message(("yf", k, i), V.at[:, PLANES - 1, some], VP.at[k, :, some], 0, 1, 0)
+
     for k in range(STEPS):
         last = k == STEPS - 1
+        send_strike(k, [0])
         fault()
         if not last:
             corners(k)
             message(("d1", k), CK.at[k], ZD1.at[k], 0, -1, 1)
             message(("d2", k), CK.at[k], ZD2.at[k], 0, 1, -1)
-        message(("yb", k), V.at[:, 0], VN.at[k], 0, -1, 0)
-        if not last:
-            message(("yf", k), V.at[:, PLANES - 1], VP.at[k], 0, 1, 0)
-        else:
-            slip_out[...] = slip[...]
-
-            def copy_plane(y):
-                for c in range(3):
-                    vel_out[c, y] = V[c, y, own]
-
-            planes(0, PLANES, copy_plane)
+        send_strike(k, [1, 2])
         pack(V, 0, 0, PK.at[k, 1], TILES, lambda y, t: not early(y, t))
         message(("zb", k), PK.at[k, 1], ZN.at[k, 1], 0, 0, -1)
         if not last:
             message(("zf", k), PK.at[k, 1], ZM.at[k, 1], 0, 0, 1)
+        if last:
+            slip_out[...] = slip[...]
+
+            def copy_plane(y):
+                for c in range(3):
+                    vel_out[c, y] = V[c, y, own]
+
+            planes(0, PLANES, copy_plane)
         if k == 0:
             arrived("zc")
             arrived("xzc")
@@ -521,35 +541,47 @@
         arrived(("zb1", k))
         unpack(ZN.at[k, 0], UN)
         planes(1, PLANES - 1, functools.partial(stress_own, k, INNER))
+        if not last:
+            arrived(("zf1", k))
+
+            @pl.when(dn_z)
+            def _():
+                unpack(ZM.at[k, 0], UM)
+                unpack(PK.at[k, 0], UO)
+                column_ghost(True)
+
+            planes(2, PLANES - 2, lambda y: trial(y, range(2, TILES - 3)))
         arrived(("zb", k))
         merge(ZN.at[k], UN)
         for y in range(1, PLANES - 1):
             stress_own(k, FAULT, y)
         stress_own(k, all_tiles, 0)
         if last:
-            arrived(("yb", k))
+            for i in range(3):
+                arrived(("yb", k, i))
             stress_last(k)
             break
-        arrived(("zf1", k))
         arrived(("zf", k))
 
         @pl.when(dn_z)
         def _():
             merge(ZM.at[k], UM)
             merge(PK.at[k], UO)
-            column_ghost()
-
-        planes(1, PLANES - 1, lambda y: trial(y, all_tiles))
+            column_ghost(False)
+
+        for y in range(2, PLANES - 2):
+            trial(y, [0, 1, TILES - 3, TILES - 2, TILES - 1])
+        planes(0, 2, lambda i: trial(1 + (PLANES - 3) * i, all_tiles))
         columns_early(k + 1)
         if k == 0:
             arrived("yc")
             arrived("xyc")
         arrived(("d1", k))
         arrived(("d2", k))
-        gone(("yb", k))
-        gone(("yf", k))
-        arrived(("yf", k))
-        arrived(("yb", k))
+        for i in range(3):
+            for name in ("yf", "yb"):
+                gone((name, k, i))
+                arrived((name, k, i))
         column_corner(k)
         stress_ghost(k)
         stress_last(k)
@@ -633,8 +665,8 @@
             pltpu.SMEM((8,), f32),
             pltpu.SMEM((8,), f32),
             pltpu.SemaphoreType.DMA((40,)),
-            pltpu.SemaphoreType.DMA((40,)),
-            pltpu.SemaphoreType.DMA((40,)),
+            pltpu.SemaphoreType.DMA((56,)),
+            pltpu.SemaphoreType.DMA((56,)),
         ],
         compiler_params=pltpu.CompilerParams(
             collective_id=0, has_side_effects=True, vmem_limit_bytes=40 * 1024 * 1024

time: 35.2 us -> 35.9 us (1.020)
  the two profiles are of different devices: /device:TPU:1 before, /device:TPU:2 now
where the time goes in v4:
time: 35.9 us; the launch traced here: 35.8 us
  Pallas kernels  35.2 us (98%)
  between operations  0.64 us (2%)
    pallas_call x1, Pallas kernels, local(): pl.pallas_call(kernel, out_shape=(jax.ShapeDtypeStruct(velocity.shape, f3...  32.9 us
    pallas_call x1, Pallas kernels, local(): pl.pallas_call(writer, out_shape=tuple((jax.ShapeDtypeStruct(x.shape, f32...  2.32 us

profile of v4, /device:TPU:2, one launch (start us, length us, event | category | flops | bytes accessed | tf_op | source)
XLA Modules:
  0.0 35.8 jit_solution(12719806888211995834)
XLA Ops:
  0.6 32.9 %rupture.1 = (f32[3,8,128,128]{3,2,1,0:T(8,128)S(1)}, f32[6,8,128,128]{3,2,1,0:T(8,128)S(1)}, f32[8,128]{1,0:T(8,128)S(1)}) custom-call(f32[3,8,128,128]{3,2,1,0:T(8,128)} %vel_hbm.1, f32[6,8,128,128]{3,2,1,0:T(8,128)} %str_hbm.1, f32[8,128,128]{2,1,0:T(8,128)} %buo_hbm.1, f32[8,128,128]{2,1,0:T(8,128)} %c11_hbm.1, f32[8,128,128]{2,1,0:T(8,128)} %c13_hbm.1, ...), custom_call_target="tpu_custom_call" | custom-call | tf_op jit(solution)/shard_map/rupture/pallas_call | solution.py:624
  33.5 2.3 %writer.1 = (f32[3,8,128,128]{3,2,1,0:T(8,128)}, f32[6,8,128,128]{3,2,1,0:T(8,128)}, f32[8,128]{1,0:T(8,128)}) custom-call(f32[3,8,128,128]{3,2,1,0:T(8,128)S(1)} %get-tuple-element.6.vel_in, f32[6,8,128,128]{3,2,1,0:T(8,128)S(1)} %get-tuple-element.7.str_in, f32[8,128]{1,0:T(8,128)S(1)} %get-tuple-element.8.slip_in), custom_call_target="tpu_custom_call" | custom-call | tf_op jit(solution)/shard_map/writer/pallas_call | solution.py:676

commit v5 on v4

--- a/solution.py
+++ b/solution.py
@@ -282,18 +282,9 @@
     def stress_ghost(k):
         stress(0, VP, lambda c: (k, c), V, lambda c: (c, 0), lambda c, t: corner_of(ZD2, k, t, c, 126), ghost=True)
 
-    def column_ghost(early):
-        in_time = jnp.logical_and(lane >= 2, lane < 12)
-        for t in range(1, TILES - 3) if early else range(TILES):
+    def column_ghost():
+        for t in range(TILES):
             r = rows(t)
-
-            def put(i, value, corner):
-                skip = lane == 14 if corner else None
-                if early:
-                    skip = jnp.logical_not(in_time)
-                elif 1 <= t < TILES - 3:
-                    skip = jnp.logical_or(in_time, skip) if corner else in_time
-                SG[i, r] = value if skip is None else jnp.where(skip, SG[i, r], value)
 
             def shifted(ref, by):
                 return pltpu.roll(ref[r], by % 128, 1)
@@ -313,12 +304,9 @@
             c13, c44, c33 = CG[0, r], CG[1, r], CG[2, r]
             zz = SG[0, r] + DT * (c13 * (exx + eyy) + c33 * ezz)
             yz = SG[2, r] + DT * c44 * ((oy - vy) + (pltpu.roll(vz, 126, 1) - vz))
-            xz = SG[1, r] + DT * c44 * ((ox - vx) + (upper_rows(2) - vz))
-            put(0, zz, True)
-            put(1, xz, False)
-            put(2, yz, True)
-            if early:
-                continue
+            SG[0, r] = jnp.where(lane == 14, SG[0, r], zz)
+            SG[1, r] = SG[1, r] + DT * c44 * ((ox - vx) + (upper_rows(2) - vz))
+            SG[2, r] = jnp.where(lane == 14, SG[2, r], yz)
             for i, value in enumerate((exx, vy, ezz, oy - vy, vz)):
                 GP[i, r] = value
 
@@ -477,6 +465,13 @@
 
     planes(1, PLANES, lambda y: trial(y, own_tiles))
 
+    def pairs(body):
+        def both(i):
+            body(2 * i + 1)
+            body(2 * i + 2)
+
+        planes(0, PLANES // 2 - 1, both)
+
     def columns_early(k):
         pack(V, 0, 0, PK.at[k, 0], TILES, early)
         message(("zb1", k), PK.at[k, 0], ZN.at[k, 0], 0, 0, -1)
@@ -540,17 +535,7 @@
             gone("y0")
         arrived(("zb1", k))
         unpack(ZN.at[k, 0], UN)
-        planes(1, PLANES - 1, functools.partial(stress_own, k, INNER))
-        if not last:
-            arrived(("zf1", k))
-
-            @pl.when(dn_z)
-            def _():
-                unpack(ZM.at[k, 0], UM)
-                unpack(PK.at[k, 0], UO)
-                column_ghost(True)
-
-            planes(2, PLANES - 2, lambda y: trial(y, range(2, TILES - 3)))
+        pairs(functools.partial(stress_own, k, INNER))
         arrived(("zb", k))
         merge(ZN.at[k], UN)
         for y in range(1, PLANES - 1):
@@ -561,17 +546,16 @@
                 arrived(("yb", k, i))
             stress_last(k)
             break
+        arrived(("zf1", k))
         arrived(("zf", k))
 
         @pl.when(dn_z)
         def _():
             merge(ZM.at[k], UM)
             merge(PK.at[k], UO)
-            column_ghost(False)
-
-        for y in range(2, PLANES - 2):
-            trial(y, [0, 1, TILES - 3, TILES - 2, TILES - 1])
-        planes(0, 2, lambda i: trial(1 + (PLANES - 3) * i, all_tiles))
+            column_ghost()
+
+        pairs(lambda y: trial(y, all_tiles))
         columns_early(k + 1)
         if k == 0:
             arrived("yc")

time: 35.9 us -> 35.2 us (0.981)
  the two profiles are of different devices: /device:TPU:2 before, /device:TPU:1 now
where the time goes in v5:
time: 35.2 us; the launch traced here: 34.6 us
  Pallas kernels  34 us (97%)
  between operations  0.64 us (2%)
    pallas_call x1, Pallas kernels, local(): pl.pallas_call(kernel, out_shape=(jax.ShapeDtypeStruct(velocity.shape, f3...  31.7 us
    pallas_call x1, Pallas kernels, local(): pl.pallas_call(writer, out_shape=tuple((jax.ShapeDtypeStruct(x.shape, f32...  2.32 us

profile of v5, /device:TPU:1, one launch (start us, length us, event | category | flops | bytes accessed | tf_op | source)
XLA Modules:
  0.0 34.6 jit_solution(2609689935425628361)
XLA Ops:
  0.6 31.7 %rupture.1 = (f32[3,8,128,128]{3,2,1,0:T(8,128)S(1)}, f32[6,8,128,128]{3,2,1,0:T(8,128)S(1)}, f32[8,128]{1,0:T(8,128)S(1)}) custom-call(f32[3,8,128,128]{3,2,1,0:T(8,128)} %vel_hbm.1, f32[6,8,128,128]{3,2,1,0:T(8,128)} %str_hbm.1, f32[8,128,128]{2,1,0:T(8,128)} %buo_hbm.1, f32[8,128,128]{2,1,0:T(8,128)} %c11_hbm.1, f32[8,128,128]{2,1,0:T(8,128)} %c13_hbm.1, ...), custom_call_target="tpu_custom_call" | custom-call | tf_op jit(solution)/shard_map/rupture/pallas_call | solution.py:608
  32.3 2.3 %writer.1 = (f32[3,8,128,128]{3,2,1,0:T(8,128)}, f32[6,8,128,128]{3,2,1,0:T(8,128)}, f32[8,128]{1,0:T(8,128)}) custom-call(f32[3,8,128,128]{3,2,1,0:T(8,128)S(1)} %get-tuple-element.6.vel_in, f32[6,8,128,128]{3,2,1,0:T(8,128)S(1)} %get-tuple-element.7.str_in, f32[8,128]{1,0:T(8,128)S(1)} %get-tuple-element.8.slip_in), custom_call_target="tpu_custom_call" | custom-call | tf_op jit(solution)/shard_map/writer/pallas_call | solution.py:660
